TPU v7x, 128 devices: a whole 4x4x4 slice. The times are simulated.
128 devices in a mesh: rep: 1, dp: 128 (over x, y, z, core).
Axes of the slice: x: 4, y: 4, z: 4, core: 2. Of those that a mesh axis runs over, the one named last changes fastest.
Arguments:
- g_w_gate: bfloat16 [128, 2, 640, 3200], P(('rep', 'dp'))
- g_w_up: bfloat16 [128, 2, 640, 3200], P(('rep', 'dp'))
- g_w_down: bfloat16 [128, 2, 3200, 640], P(('rep', 'dp'))
- w_gate: bfloat16 [2, 640, 3200], replicated
- w_up: bfloat16 [2, 640, 3200], replicated
- w_down: bfloat16 [2, 3200, 640], replicated
- m_w_gate: float32 [2, 640, 3200], P(None, 'dp')
- m_w_up: float32 [2, 640, 3200], P(None, 'dp')
- m_w_down: float32 [2, 3200, 640], P(None, 'dp')
- v_w_gate: float32 [2, 640, 3200], P(None, 'dp')
- v_w_up: float32 [2, 640, 3200], P(None, 'dp')
- v_w_down: float32 [2, 3200, 640], P(None, 'dp')
Outputs:
- output 1: bfloat16 [2, 640, 3200], P('rep')
- output 2: bfloat16 [2, 640, 3200], P('rep')
- output 3: bfloat16 [2, 3200, 640], P('rep')
- output 4: float32 [2, 640, 3200], P('rep', 'dp')
- output 5: float32 [2, 640, 3200], P('rep', 'dp')
- output 6: float32 [2, 3200, 640], P('rep', 'dp')
- output 7: float32 [2, 640, 3200], P('rep', 'dp')
- output 8: float32 [2, 640, 3200], P('rep', 'dp')
- output 9: float32 [2, 3200, 640], P('rep', 'dp')
All inputs are finite; a program needn't handle non-finite values.
Results may differ from a plain program's by a relative error of at most 0.022.
Values are sent between devices in bfloat16 or wider.
A program may use at most 1.5 GiB of HBM per device.

v0:
```python
import jax
import jax.numpy as jnp
from jax import lax
from jax.sharding import PartitionSpec as P


def adamw(w, m, v, g):
    m = 0.9 * m + 0.1 * g
    v = 0.95 * v + 0.05 * g * g
    step = m * lax.rsqrt(v + 1e-8) + 0.1 * w
    return (w - 0.02 * step).astype(jnp.bfloat16), m, v


def solution(mesh):
    def step(*arrays):
        terms, weights, m, v = (arrays[i : i + 3] for i in (0, 3, 6, 9))
        gradients = [lax.psum_scatter(t[0], "dp", scatter_dimension=1, tiled=True).astype(jnp.float32) for t in terms]
        me = lax.axis_index("dp")
        own = [lax.dynamic_slice_in_dim(w, me * one.shape[1], one.shape[1], 1).astype(jnp.float32) for w, one in zip(weights, m, strict=True)]
        new = [adamw(w, m, v, g) for w, m, v, g in zip(own, m, v, gradients, strict=True)]
        whole = [lax.all_gather(one[0], "dp", axis=1, tiled=True) for one in new]
        return (*whole, *(one[1] for one in new), *(one[2] for one in new))

    all_of, cut = P(None, None, None), P(None, "dp", None)
    return jax.shard_map(
        step,
        mesh=mesh,
        in_specs=(P(("rep", "dp"), None, None, None),) * 3 + (all_of,) * 3 + (cut,) * 6,
        out_specs=(P("rep", None, None),) * 3 + (P("rep", "dp", None),) * 6,
        check_vma=False,
    )
```

profile of v0, /device:TPU:1, one launch (start us, length us, event | category | flops | bytes accessed | tf_op | source)
XLA Modules:
  0.0 543.8 jit_solution(13250696341166351557)
XLA Ops:
  7.2 0.0 all-reduce.6.cloned.1.call-start
  7.2 0.0 copy-start
  7.2 0.0 copy-start.1
  7.2 38.5 %copy.48 = bf16[1,2,3200,640]{3,1,2,0:T(2,128)(2,1)} copy(bf16[1,2,3200,640]{3,2,1,0:T(8,128)(2,1)} %param.14) | data formatting | bytes 16384000 | tf_op args[2]
  45.8 0.0 copy-done
  45.8 40.0 %copy_bitcast_fusion.1 = (bf16[2,640,3200]{2,0,1:T(2,128)(2,1)}, bf16[2,640,3200]{2,0,1:T(2,128)(2,1)}) fusion(bf16[1,2,640,3200]{3,2,1,0:T(8,128)(2,1)S(1)} %copy-done, bf16[1,2,640,3200]{3,2,1,0:T(8,128)(2,1)S(1)} %copy-done.1), kind=kLoop, calls=%fused_computation.1 | loop fusion | bytes 32768000 | tf_op jit(solution)/shard_map/squeeze | solution.py:17
  85.8 0.0 copy-start.4
  85.8 0.0 copy-start.5
  85.8 0.0 copy-start.6
  85.8 0.0 copy-start.7
  85.8 0.0 all-reduce.6.cloned.1.call-update
  85.8 0.0 all-gather.6.cloned.1.call-start
  85.9 1.3 constant_dynamic-slice_fusion.1
  87.2 230.2 %all-reduce.6.cloned.1.call-done = (bf16[2,640,3200]{2,0,1:T(2,128)(2,1)}, bf16[2,640,3200]{2,0,1:T(2,128)(2,1)}, bf16[2,3200,640]{2,0,1:T(2,128)(2,1)}) async-done(((bf16[2,640,3200]{2,0,1:T(2,128)(2,1)}, bf16[2,640,3200]{2,0,1:T(2,128)(2,1)}, bf16[2,3200,640]{2,0,1:T(2,128)(2,1)}), (bf16[2,640,3200]{2,0,1:T(2,128)(2,1)}, bf16[2,640,3200]{2,0,1:T(2,128)(2,1)}, ...) | async-done | bytes 24576016
  317.3 0.0 copy-done.3
  317.3 1.9 fusion.13
  319.2 0.0 all-gather.6.cloned.1.call-update
  319.2 0.0 all-gather.4.cloned.1.call-start
  319.3 1.9 fusion.12
  321.2 0.0 all-gather.4.cloned.1.call-update
  321.2 0.0 all-gather.8.cloned.1.call-start
  321.3 0.9 constant_dynamic-slice_fusion
  322.2 0.0 copy-done.6
  322.2 0.0 copy-done.7
  322.2 1.9 fusion.14
  324.1 0.0 all-gather.8.cloned.1.call-update
  324.1 64.9 %all-gather.6.cloned.1.call-done = bf16[2,640,3200]{2,0,1:T(2,128)(2,1)} async-done(((bf16[2,5,3200]{2,0,1:T(2,128)(2,1)}), bf16[2,640,3200]{2,0,1:T(2,128)(2,1)}) %all-gather.6.cloned.1.call-update) | async-done | bytes 8192016 | tf_op jit(solution)/shard_map/all_gather | solution.py:21
  389.0 7.6 %copy.37 = bf16[2,640,3200]{2,1,0:T(8,128)(2,1)} copy(bf16[2,640,3200]{2,0,1:T(2,128)(2,1)} %all-gather.6.cloned.1.call-done) | data formatting | bytes 16384000
  396.6 63.0 %all-gather.4.cloned.1.call-done = bf16[2,640,3200]{2,0,1:T(2,128)(2,1)} async-done(((bf16[2,5,3200]{2,0,1:T(2,128)(2,1)}), bf16[2,640,3200]{2,0,1:T(2,128)(2,1)}) %all-gather.4.cloned.1.call-update) | async-done | bytes 8192016 | tf_op jit(solution)/shard_map/all_gather | solution.py:21
  459.7 7.6 %copy.36 = bf16[2,640,3200]{2,1,0:T(8,128)(2,1)} copy(bf16[2,640,3200]{2,0,1:T(2,128)(2,1)} %all-gather.4.cloned.1.call-done) | data formatting | bytes 16384000
  467.3 62.3 %all-gather.8.cloned.1.call-done = bf16[2,3200,640]{2,0,1:T(2,128)(2,1)} async-done(((bf16[2,25,640]{2,0,1:T(2,128)(2,1)}), bf16[2,3200,640]{2,0,1:T(2,128)(2,1)}) %all-gather.8.cloned.1.call-update) | async-done | bytes 8192016 | tf_op jit(solution)/shard_map/all_gather | solution.py:21
  529.6 7.7 %copy.38 = bf16[2,3200,640]{2,1,0:T(8,128)(2,1)} copy(bf16[2,3200,640]{2,0,1:T(2,128)(2,1)} %all-gather.8.cloned.1.call-done) | data formatting | bytes 16384000
  (6 shorter events, 0.0 us)
Async XLA Ops:
  7.2 310.2 %all-reduce.6.cloned.1.call-start = ((), (), s32[]{:S(2)}) async-start(), calls=%async_computation.3 | async-start | bytes 49152000
  7.2 38.5 %copy-start = (bf16[1,2,640,3200]{3,2,1,0:T(8,128)(2,1)S(1)}, bf16[1,2,640,3200]{3,2,1,0:T(8,128)(2,1)}, u32[]{:S(2)}) copy-start(bf16[1,2,640,3200]{3,2,1,0:T(8,128)(2,1)} %param.13) | copy-start | bytes 24576004
  7.2 38.5 %copy-start.1 = (bf16[1,2,640,3200]{3,2,1,0:T(8,128)(2,1)S(1)}, bf16[1,2,640,3200]{3,2,1,0:T(8,128)(2,1)}, u32[]{:S(2)}) copy-start(bf16[1,2,640,3200]{3,2,1,0:T(8,128)(2,1)} %param.12) | copy-start | bytes 24576004
  85.7 231.6 %copy-start.2 = (f32[2,5,3200]{2,0,1:T(2,128)S(1)}, f32[2,5,3200]{2,0,1:T(2,128)}, u32[]{:S(2)}) copy-start(f32[2,5,3200]{2,0,1:T(2,128)} %param.22) | copy-start | bytes 384004
  85.7 231.6 %copy-start.3 = (f32[2,5,3200]{2,0,1:T(2,128)S(1)}, f32[2,5,3200]{2,0,1:T(2,128)}, u32[]{:S(2)}) copy-start(f32[2,5,3200]{2,0,1:T(2,128)} %param.19) | copy-start | bytes 384004
  85.8 233.5 %copy-start.4 = (f32[2,5,3200]{2,0,1:T(2,128)S(1)}, f32[2,5,3200]{2,0,1:T(2,128)}, u32[]{:S(2)}) copy-start(f32[2,5,3200]{2,0,1:T(2,128)} %param.21) | copy-start | bytes 384004
  85.8 233.5 %copy-start.5 = (f32[2,5,3200]{2,0,1:T(2,128)S(1)}, f32[2,5,3200]{2,0,1:T(2,128)}, u32[]{:S(2)}) copy-start(f32[2,5,3200]{2,0,1:T(2,128)} %param.18) | copy-start | bytes 384004
  85.8 236.4 %copy-start.6 = (f32[2,25,640]{2,0,1:T(2,128)S(1)}, f32[2,25,640]{2,0,1:T(2,128)}, u32[]{:S(2)}) copy-start(f32[2,25,640]{2,0,1:T(2,128)} %param.23) | copy-start | bytes 384004
  85.8 236.4 %copy-start.7 = (f32[2,25,640]{2,0,1:T(2,128)S(1)}, f32[2,25,640]{2,0,1:T(2,128)}, u32[]{:S(2)}) copy-start(f32[2,25,640]{2,0,1:T(2,128)} %param.20) | copy-start | bytes 384004
  85.8 303.2 %all-gather.6.cloned.1.call-start = ((), (), s32[]{:S(2)}) async-start(), calls=%async_computation.1 | async-start | bytes 8256000 | tf_op jit(solution)/shard_map/all_gather | solution.py:21
  319.2 140.4 %all-gather.4.cloned.1.call-start = ((), (), s32[]{:S(2)}) async-start(), calls=%async_computation | async-start | bytes 8256000 | tf_op jit(solution)/shard_map/all_gather | solution.py:21
  321.2 208.4 %all-gather.8.cloned.1.call-start = ((), (), s32[]{:S(2)}) async-start(), calls=%async_computation.2 | async-start | bytes 8256000 | tf_op jit(solution)/shard_map/all_gather | solution.py:21
Sparse Core Ops, SparseCore 0:
  85.9 231.3 all-reduce.5
  320.9 68.0 all-gather.5
  392.5 67.0 all-gather.3
  462.5 67.0 all-gather.7
where the time goes:
time: 544 us
  waiting for transfers between devices  420 us (77%)
  local copies, waits for them, and re-layouts  104 us (19%)
  between operations  13.9 us (3%)
  other arithmetic  5.64 us (1%)
    unnamed x5, waiting for transfers between devices  230 us
    all_gather x3, waiting for transfers between devices, step(): whole = [lax.all_gather(one[0], 'dp', axis=1, tiled=True) for one in new]  190 us
    unnamed x20, local copies, waits for them, and re-layouts  61.5 us
    squeeze x1, local copies, waits for them, and re-layouts, step(): t[0]  40 us
  transfers between devices with their start and end apart: 4, of which 4 were waited for; matrix products, arithmetic and copies ran while one was open for 4% of the time, Pallas kernels for 0%

commit v1 on v0

v1 whole, which is shorter than its diff:
```python
import jax
import jax.numpy as jnp
from jax import lax
from jax.experimental import pallas as pl
from jax.experimental.pallas import tpu as pltpu
from jax.sharding import PartitionSpec as P

BF, F32 = jnp.bfloat16, jnp.float32
WA = 3328
WC = 768
OFF = (2, 3, 1, 0)
HBM = pltpu.MemorySpace.HBM
VMEM = pltpu.MemorySpace.VMEM


def adamw(w, m, v, g):
    m = 0.9 * m + 0.1 * g
    v = 0.95 * v + 0.05 * g * g
    step = m * lax.rsqrt(v + 1e-8) + 0.1 * w
    return (w - 0.02 * step).astype(jnp.bfloat16), m, v


class Place:
    def __init__(self):
        me = lax.axis_index("dp")
        self.c = lax.rem(me, 2)
        self.z = lax.rem(me // 2, 4)
        self.y = lax.rem(me // 8, 4)
        self.x = me // 32
        self.g = lax.rem(me, 8)
        self.partner = self.dev(c=1 - self.c)

    def dev(self, x=None, y=None, z=None, c=None):
        x = self.x if x is None else x
        y = self.y if y is None else y
        z = self.z if z is None else z
        c = self.c if c is None else c
        return {"dp": ((x * 4 + y) * 4 + z) * 2 + c}

    def step(self, dim, by):
        return self.dev(**{dim: lax.rem(getattr(self, dim) + by, 4)})

    def group(self):
        out = [(self.z, 1 - self.c)]
        for dz in (1, 2, 3):
            zz = lax.rem(self.z + dz, 4)
            out += [(zz, self.c), (zz, 1 - self.c)]
        return out

    def barrier(self):
        sem = pltpu.get_barrier_semaphore()
        peers = [self.dev(z=z, c=c) for z, c in self.group()]
        peers += [self.step(d, by) for d in ("x", "y") for by in (1, 3)]
        for peer in peers:
            pl.semaphore_signal(sem, inc=1, device_id=peer, device_id_type=pl.DeviceIdType.MESH)
        pl.semaphore_wait(sem, len(peers))


class Sender:
    def __init__(self, send, recv):
        self.send, self.recv, self.n, self.all = send, recv, 0, []

    def start(self, src, dst, device):
        copy = pltpu.make_async_remote_copy(
            src_ref=src,
            dst_ref=dst,
            send_sem=self.send.at[self.n],
            recv_sem=self.recv.at[self.n],
            device_id=device,
            device_id_type=pl.DeviceIdType.MESH,
        )
        copy.start()
        self.n += 1
        self.all.append(copy)
        return copy

    def drain(self):
        for copy in self.all:
            copy.wait_send()


def rows(start, n):
    return pl.ds(pl.multiple_of(start, 8), n)


def total(refs, sl):
    acc = refs[0][sl].astype(F32)
    for r in refs[1:]:
        acc = acc + r[sl].astype(F32)
    return acc


def vadd(dst, refs, n, step):
    def body(i, carry):
        sl = (rows(i * step, step), slice(None))
        dst[sl] = total(refs, sl).astype(dst.dtype)
        return carry

    lax.fori_loop(0, n // step, body, 0)


def interleave(*programs):
    live = list(programs)
    while live:
        for p in list(live):
            try:
                next(p)
            except StopIteration:
                live.remove(p)


def reduce_kernel(g_gate, g_up, g_down, o_gate, o_up, o_down, own_a, par_a, own_b, par_b, own_c, par_c, r1a, r2a, r1b, r2b, r1c, r2c,
                  s1a, s2a, s1b, s2b, s1c, s2c, t1c, t2c, f_a, f_b, f_c, snd_a, snd_b, snd_c, rcv_a, rcv_b, rcv_c, send, recv, local):
    at = Place()
    x, y, z, c = at.x, at.y, at.z, at.c
    net = Sender(send, recv)
    loads = [0]

    rel = lambda base, j: lax.rem(base + OFF[j], 4)

    def item_a(ref, k, j):
        return ref.at[rows(160 * k + 40 * rel(y, j), 40), :]

    def item_b(ref, k, j):
        return ref.at[rows(200 * k + 800 * rel(x, j), 200), :]

    def item_c(ref, k, j):
        return ref.at[k, rows(160 * rel(x, j), 160), :]

    def src_a(layer, k, j):
        return g_up.at[0, layer, rows(160 * k + 40 * rel(y, j), 40), :]

    def src_b(layer, k, j):
        return g_down.at[0, layer, rows(200 * k + 800 * rel(x, j), 200), :]

    def src_c(layer, k, j):
        return g_gate.at[0, layer, rows(160 * rel(x, j), 160), pl.ds(pl.multiple_of(WC * k, 128), WC)]

    def dst_a(ref, k, j):
        return ref.at[rows(160 * k + 40 * rel(y, j), 40), pl.ds(0, 3200)]

    colours = {
        "a": (own_a, par_a, item_a, src_a, dst_a, x, "x", r1a, r2a, 40, 8),
        "b": (own_b, par_b, item_b, src_b, item_b, y, "y", r1b, r2b, 200, 40),
        "c": (own_c, par_c, item_c, src_c, item_c, z, "z", r1c, r2c, 160, 32),
    }

    def load(src, dst):
        copy = pltpu.make_async_copy(src, dst, local.at[loads[0]])
        copy.start()
        loads[0] += 1
        return copy

    near = {}
    tail = (0, c, slice(None), pl.ds(3072, 128))
    near["tail"] = load(g_gate.at[tail], own_a.at[:, pl.ds(3200, 128)])
    order = [(2, j) for j in (0, 2, 1, 3)] + [(1, 2), (3, 0), (1, 3), (3, 1), (1, 0), (3, 2), (1, 1), (3, 3)] + [(0, j) for j in (0, 2, 1, 3)]
    for dk, j in order:
        for n, (own, par, item, src, dst, k0, *_) in colours.items():
            k = lax.rem(k0 + dk, 4)
            near[n, dk, j] = load(src(c, k, j), dst(own, k, j))
    at.barrier()
    far = {}
    tail = (0, 1 - c, slice(None), pl.ds(3072, 128))
    far["tail"] = net.start(g_gate.at[tail], par_a.at[:, pl.ds(3200, 128)], at.partner)
    for dk, j in order:
        for n, (own, par, item, src, dst, k0, *_) in colours.items():
            k = lax.rem(k0 + dk, 4)
            far[n, dk, j] = net.start(src(1 - c, k, j), dst(par, k, j), at.partner)
    near["tail"].wait()
    far["tail"].wait_recv()

    def first(n):
        own, par, item, src, dst, k0, dim, r1, r2, height, step = colours[n]
        up, down = at.step(dim, 1), at.step(dim, 3)
        k2, kp, km = (lax.rem(k0 + d, 4) for d in (2, 1, 3))
        one, two = {}, {}
        for j in (0, 2, 1, 3):
            yield
            near[n, 2, j].wait()
            far[n, 2, j].wait_recv()
            here = item(own, k2, j)
            vadd(here, (here, item(par, k2, j)), height, step)
            one[j] = net.start(here, r1.at[j], up if j < 2 else down)
        for dk, j in ((1, 2), (3, 0), (1, 3), (3, 1)):
            yield
            near[n, dk, j].wait()
            far[n, dk, j].wait_recv()
            k = kp if dk == 1 else km
            here = item(own, k, j)
            vadd(here, (here, item(par, k, j)), height, step)
            two[dk, j] = net.start(here, r2.at[j if dk == 1 else 4 + j], up if dk == 1 else down)
        for dk, j in ((1, 0), (3, 2), (1, 1), (3, 3)):
            yield
            near[n, dk, j].wait()
            far[n, dk, j].wait_recv()
            one[j].wait_recv()
            k = kp if dk == 1 else km
            here = item(own, k, j)
            vadd(here, (here, item(par, k, j), r1.at[j]), height, step)
            two[dk, j] = net.start(here, r2.at[j if dk == 1 else 4 + j], up if dk == 1 else down)
        for j in (0, 2, 1, 3):
            yield
            near[n, 0, j].wait()
            far[n, 0, j].wait_recv()
            two[1, j].wait_recv()
            two[3, j].wait_recv()
            here = item(own, k0, j)
            vadd(here, (here, item(par, k0, j), r2.at[j], r2.at[4 + j]), height, step)
            yield j

    def later(n, dim, block, halves, r1, r2, ready, step, done):
        up, down = at.step(dim, 1), at.step(dim, 3)
        two = {}
        for j in ready:
            yield
            if j == 0:
                a = net.start(halves(block(0), 0), halves(r1.at[0], 0, True), up)
                b = net.start(halves(block(0), 1), halves(r1.at[1], 1, True), down)
            if j == 2:
                two[0] = net.start(halves(block(2), 1), halves(r2.at[0], 1), up)
            if j == 1:
                two[1] = net.start(halves(block(1), 0), halves(r2.at[1], 0), down)
        yield
        a.wait_recv()
        here = halves(block(2), 0)
        vadd(here, (here, halves(r1.at[0], 0, True)), here.shape[0], 8)
        two[2] = net.start(here, halves(r2.at[0], 0), up)
        yield
        b.wait_recv()
        here = halves(block(1), 1)
        vadd(here, (here, halves(r1.at[1], 1, True)), here.shape[0], 8)
        two[3] = net.start(here, halves(r2.at[1], 1), down)
        yield
        for i in range(4):
            two[i].wait_recv()
        vadd(done, (block(3), r2.at[0], r2.at[1]), block(3).shape[0], step)
        yield

    def steps(gen):
        for j in gen:
            yield j

    def halves_cols(w):
        def cut(ref, h, packed=False):
            return ref if packed else ref.at[:, pl.ds(h * w, w)]

        return cut

    def halves_rows(n0, n1):
        def cut(ref, h, packed=False):
            return ref.at[pl.ds(0, (n0, n1)[h]), :] if packed else ref.at[pl.ds((0, n0)[h], (n0, n1)[h]), :]

        return cut

    def spread(n, full, blocks, height, snd, rcv):
        sent = []
        for k in range(8):
            snd[k] = full[pl.ds(blocks * k, height), :].astype(BF)
        for zz, cc in at.group():
            s = 2 * zz + cc
            sent.append(net.start(snd.at[s], rcv.at[at.g], at.dev(z=zz, c=cc)))
        rcv[at.g] = snd[at.g]
        return sent

    sent = {}

    def colour_a():
        f_a[pl.ds(40, 8), :] = jnp.zeros((8, WA), F32)
        yield from later("a", "y", lambda j: item_a(own_a, x, j), halves_cols(WA // 2), s1a, s2a, first("a"), 8, f_a)
        sent["a"] = spread("a", f_a, 5, 8, snd_a, rcv_a)

    def colour_b():
        f_b[pl.ds(200, 8), :] = jnp.zeros((8, 640), F32)
        yield from later("b", "x", lambda j: item_b(own_b, y, j), halves_rows(104, 96), s1b, s2b, first("b"), 40, f_b)
        sent["b"] = spread("b", f_b, 25, 32, snd_b, rcv_b)

    def colour_c():
        f_c[pl.ds(40, 8), :] = jnp.zeros((8, WC), F32)
        yield from later("c", "x", lambda j: item_c(own_c, z, j), halves_rows(80, 80), s1c, s2c, first("c"), 32, item_c(own_c, z, 3))
        block = lambda j: own_c.at[z, rows(160 * x + 40 * rel(y, j), 40), :]
        yield from later("c", "y", block, halves_cols(WC // 2), t1c, t2c, iter((0, 2, 1, 3)), 8, f_c)
        sent["c"] = spread("c", f_c, 5, 8, snd_c, rcv_c)

    interleave(colour_a(), colour_b(), colour_c())

    for n in ("a", "b", "c"):
        for copy in sent[n]:
            copy.wait_recv()
    for layer in range(2):
        acc = rcv_a[layer].astype(F32)
        low = rcv_b[layer].astype(F32)
        for zz in range(1, 4):
            acc = acc + rcv_a[2 * zz + layer].astype(F32)
            low = low + rcv_b[2 * zz + layer].astype(F32)
        o_up[layer] = acc[:, :3200].astype(BF)
        o_gate[layer, :, pl.ds(3072, 128)] = acc[:, 3200:].astype(BF)
        o_down[layer] = low.astype(BF)
        for zz in range(4):
            o_gate[layer, :, pl.ds(WC * zz, WC)] = rcv_c[2 * zz + layer]
    net.drain()


def gather_kernel(w_a, w_b, w_c, o_a, o_b, o_c, g_a, g_b, g_c, f_a, f_b, f_c, send, recv):
    at = Place()
    x, y, z, c = at.x, at.y, at.z, at.c
    net = Sender(send, recv)
    at.barrier()
    rel = lambda base, j: lax.rem(base + OFF[j], 4)
    cross = []

    def window(zz):
        return pl.ds(pl.multiple_of(WC * zz, 128), WC)

    sent = {"a": [], "b": [], "c": []}
    for zz, cc in at.group():
        device = at.dev(z=zz, c=cc)
        sent["c"].append(net.start(w_c.at[cc, :, window(zz)], g_c.at[at.g], device))
        sent["a"].append(net.start(w_a.at[cc], g_a.at[at.g], device))
        sent["b"].append(net.start(w_b.at[cc], g_b.at[at.g], device))
    g_c[at.g] = w_c[c, :, window(z)]
    g_a[at.g] = w_a[c]
    g_b[at.g] = w_b[c]

    def over(ref):
        cross.append(net.start(ref, ref, at.partner))

    def build(n, blocks, got, full, out):
        for copy in sent[n]:
            copy.wait_recv()
        for k in range(8):
            full[pl.ds(blocks * k, blocks), :] = got[k].astype(F32)[:blocks]
        out[...] = full[...].astype(BF)

    def small(dim, block, halves):
        up, down = at.step(dim, 1), at.step(dim, 3)
        mine = block(3)
        m0 = net.start(halves(mine, 0), halves(mine, 0), up)
        p1 = net.start(halves(mine, 1), halves(mine, 1), down)
        m1 = net.start(halves(mine, 1), halves(mine, 1), up)
        p0 = net.start(halves(mine, 0), halves(mine, 0), down)
        yield 3
        m0.wait_recv()
        here = halves(block(1), 0)
        f0 = net.start(here, here, up)
        p1.wait_recv()
        here = halves(block(2), 1)
        f1 = net.start(here, here, down)
        yield
        m1.wait_recv()
        yield 1
        p0.wait_recv()
        yield 2
        f0.wait_recv()
        f1.wait_recv()
        yield 0

    def large(dim, k0, item, ready):
        up, down = at.step(dim, 1), at.step(dim, 3)
        kp, km, k2 = (lax.rem(k0 + d, 4) for d in (1, 3, 2))
        fm, fp, order = {}, {}, []
        for j in ready:
            if j is not None:
                here = item(k0, j)
                fm[j] = net.start(here, here, up)
                fp[j] = net.start(here, here, down)
                over(here)
                order.append(j)
            yield
        f2 = {}
        for j in order:
            fm[j].wait_recv()
            here = item(km, j)
            if j < 2:
                f2[j] = net.start(here, here, up)
            over(here)
            yield
            fp[j].wait_recv()
            here = item(kp, j)
            if j >= 2:
                f2[j] = net.start(here, here, down)
            over(here)
            yield
        for j in order:
            f2[j].wait_recv()
            over(item(k2, j))
            yield

    def cols(w):
        return lambda ref, h: ref.at[:, pl.ds(h * w, w)]

    def parts(n0, n1):
        return lambda ref, h: ref.at[pl.ds((0, n0)[h], (n0, n1)[h]), :]

    item_a = lambda k, j: o_a.at[c, rows(160 * k + 40 * rel(y, j), 40), :]
    item_b = lambda k, j: o_b.at[c, rows(200 * k + 800 * rel(x, j), 200), :]
    item_c = lambda k, j: o_c.at[c, k, rows(160 * rel(x, j), 160), :]

    def colour_a():
        build("a", 5, g_a, f_a, item_a(x, 3))
        yield from large("x", x, item_a, small("y", lambda j: item_a(x, j), cols(WA // 2)))

    def colour_b():
        build("b", 25, g_b, f_b, item_b(y, 3))
        yield from large("y", y, item_b, small("x", lambda j: item_b(y, j), parts(104, 96)))

    def colour_c():
        block = lambda j: o_c.at[c, z, rows(160 * x + 40 * rel(y, j), 40), :]
        build("c", 5, g_c, f_c, block(3))
        for _ in small("y", block, cols(WC // 2)):
            yield
        yield from large("z", z, item_c, small("x", lambda j: item_c(z, j), parts(80, 80)))

    interleave(colour_c(), colour_a(), colour_b())
    for copy in cross:
        copy.wait_recv()
    net.drain()


def write_kernel(a, b, c, gate, up, down, sem):
    copies = [(b.at[l], down.at[l]) for l in range(2)]
    copies += [(a.at[l, :, pl.ds(0, 3200)], up.at[l]) for l in range(2)]
    copies += [(c.at[l, k], gate.at[l, :, pl.ds(WC * k, WC)]) for l in range(2) for k in range(4)]
    copies += [(a.at[l, :, pl.ds(3200, 128)], gate.at[l, :, pl.ds(3072, 128)]) for l in range(2)]
    copies = [pltpu.make_async_copy(s, d, sem.at[i]) for i, (s, d) in enumerate(copies)]
    for copy in copies:
        copy.start()
    for copy in copies:
        copy.wait()


def spec(space, n):
    return [pl.BlockSpec(memory_space=space)] * n


def solution(mesh):
    def step(*arrays):
        terms, weights, m, v = (arrays[i : i + 3] for i in (0, 3, 6, 9))
        sums = pl.pallas_call(
            reduce_kernel,
            out_shape=[VMEM((2, 8, 3200), BF), VMEM((2, 8, 3200), BF), VMEM((2, 32, 640), BF)],
            in_specs=spec(HBM, 3),
            out_specs=spec(VMEM, 3),
            scratch_shapes=[
                *[VMEM((640, WA), BF)] * 2,
                *[VMEM((3200, 640), BF)] * 2,
                *[VMEM((4, 640, WC), BF)] * 2,
                *[VMEM((n, *s), BF) for s in ((40, WA), (200, 640), (160, WC)) for n in (4, 8)],
                VMEM((2, 40, WA // 2), BF),
                VMEM((2, 40, WA), BF),
                VMEM((2, 104, 640), BF),
                VMEM((2, 200, 640), BF),
                VMEM((2, 80, WC), BF),
                VMEM((2, 160, WC), BF),
                VMEM((2, 40, WC // 2), BF),
                VMEM((2, 40, WC), BF),
                VMEM((48, WA), F32),
                VMEM((208, 640), F32),
                VMEM((48, WC), F32),
                *[VMEM((8, *s), BF) for s in ((8, WA), (32, 640), (8, WC))] * 2,
                pltpu.SemaphoreType.DMA((140,)),
                pltpu.SemaphoreType.DMA((140,)),
                pltpu.SemaphoreType.DMA((49,)),
            ],
            compiler_params=pltpu.CompilerParams(collective_id=0, has_side_effects=True, vmem_limit_bytes=56 * 2**20),
            name="reduce",
        )(*terms)
        gradients = [s[:, : one.shape[1]].astype(F32) for s, one in zip(sums, m, strict=True)]
        me = lax.axis_index("dp")
        own = [lax.dynamic_slice_in_dim(w, me * one.shape[1], one.shape[1], 1).astype(F32) for w, one in zip(weights, m, strict=True)]
        new = [adamw(w, m, v, g) for w, m, v, g in zip(own, m, v, gradients, strict=True)]
        gate, up, down = (one[0] for one in new)
        w_a = jnp.pad(jnp.concatenate([up, gate[:, :, 3072:]], 2), ((0, 0), (0, 3), (0, 0)))
        w_b = jnp.pad(down, ((0, 0), (0, 7), (0, 0)))
        w_c = jnp.pad(gate[:, :, :3072], ((0, 0), (0, 3), (0, 0)))
        whole = pl.pallas_call(
            gather_kernel,
            out_shape=[VMEM((2, 640, WA), BF), VMEM((2, 3200, 640), BF), VMEM((2, 4, 640, WC), BF)],
            in_specs=spec(VMEM, 3),
            out_specs=spec(VMEM, 3),
            scratch_shapes=[
                VMEM((8, 8, WA), BF),
                VMEM((8, 32, 640), BF),
                VMEM((8, 8, WC), BF),
                VMEM((40, WA), F32),
                VMEM((200, 640), F32),
                VMEM((40, WC), F32),
                pltpu.SemaphoreType.DMA((140,)),
                pltpu.SemaphoreType.DMA((140,)),
            ],
            compiler_params=pltpu.CompilerParams(collective_id=1, has_side_effects=True, vmem_limit_bytes=8 * 2**20),
            name="gather",
        )(w_a, w_b, w_c)
        whole = pl.pallas_call(
            write_kernel,
            out_shape=[jax.ShapeDtypeStruct(w.shape, BF) for w in weights],
            in_specs=spec(VMEM, 3),
            out_specs=spec(HBM, 3),
            scratch_shapes=[pltpu.SemaphoreType.DMA((14,))],
            compiler_params=pltpu.CompilerParams(vmem_limit_bytes=2**20),
            name="write",
        )(*whole)
        return (*whole, *(one[1] for one in new), *(one[2] for one in new))

    all_of, cut = P(None, None, None), P(None, "dp", None)
    return jax.shard_map(
        step,
        mesh=mesh,
        in_specs=(P(("rep", "dp"), None, None, None),) * 3 + (all_of,) * 3 + (cut,) * 6,
        out_specs=(P("rep", None, None),) * 3 + (P("rep", "dp", None),) * 6,
        check_vma=False,
    )
```

time: 544 us -> 179 us (0.33)
  waiting for transfers between devices: 420 us -> 0 us
  Pallas kernels: 0 us -> 171 us
  local copies, waits for them, and re-layouts: 104 us -> 4.43 us
  between operations: 13.9 us -> 0.77 us
    unnamed x5 -> x0, waiting for transfers between devices: 230 us -> none
    all_gather x3 -> x0, waiting for transfers between devices: 190 us -> none  [step(): whole = [lax.all_gather(one[0], 'dp', axis=1, tiled=True) for one in new]]
    pallas_call x0 -> x3, Pallas kernels: none -> 171 us  [the longest x1 85.2 us: step(): pl.pallas_call(gather_kernel, out_shape=[VMEM((2, 640, WA), BF), VMEM((2,...]
    unnamed x20 -> x18, local copies, waits for them, and re-layouts: 61.5 us -> 4.39 us
    squeeze x1 -> x0, local copies, waits for them, and re-layouts: 40 us -> none  [step(): t[0]]
  transfers between devices with their start and end apart: 4 -> 0, of which waited for: 4 -> 0; matrix products, arithmetic and copies ran while one was open for 4% -> 0% of each run, Pallas kernels for 0% -> 0%
where the time goes in v1:
time: 179 us
  Pallas kernels  171 us (96%)
  local copies, waits for them, and re-layouts  4.43 us (2%)
  other arithmetic  2.38 us (1%)
    pallas_call x1, Pallas kernels, step(): pl.pallas_call(gather_kernel, out_shape=[VMEM((2, 640, WA), BF), VMEM((2,...  85.2 us
    pallas_call x1, Pallas kernels, step(): pl.pallas_call(reduce_kernel, out_shape=[VMEM((2, 8, 3200), BF), VMEM((2,...  77.3 us
    pallas_call x1, Pallas kernels, step(): pl.pallas_call(write_kernel, out_shape=[jax.ShapeDtypeStruct(w.shape, BF)...  8.36 us
    unnamed x18, local copies, waits for them, and re-layouts  4.39 us

profile of v1, /device:TPU:1, one launch (start us, length us, event | category | flops | bytes accessed | tf_op | source)
XLA Modules:
  0.0 178.5 jit_solution(11879292798061297224)
XLA Ops:
  0.6 0.0 copy-start.4
  0.7 0.0 copy-start.5
  0.7 0.0 copy-start
  0.7 0.0 copy-start.1
  0.7 0.0 copy-start.2
  0.7 0.0 copy-start.3
  0.7 77.3 %reduce.1 = (bf16[2,8,3200]{2,1,0:T(8,128)(2,1)S(1)}, bf16[2,8,3200]{2,1,0:T(8,128)(2,1)S(1)}, bf16[2,32,640]{2,1,0:T(8,128)(2,1)S(1)}) custom-call(bf16[1,2,640,3200]{3,2,1,0:T(8,128)(2,1)} %g_gate.1, bf16[1,2,640,3200]{3,2,1,0:T(8,128)(2,1)} %g_up.1, bf16[1,2,3200,640]{3,2,1,0:T(8,128)(2,1)} %g_down.1), custom_call_target="tpu_custom_call" | custom-call | tf_op jit(solution)/shard_map/reduce/pallas_call | solution.py:439
  78.1 0.0 copy-done.4
  78.1 0.0 copy-done.5
  78.1 1.0 fusion.14
  79.1 0.8 copy.32
  79.9 0.7 copy.29
  80.6 0.0 copy-done
  80.6 0.0 copy-done.1
  80.6 0.0 copy-done.2
  80.6 0.0 copy-done.3
  80.6 1.3 fusion.4
  82.1 0.7 copy.31
  82.8 0.7 copy.28
  83.5 0.7 copy.30
  84.2 0.7 copy.27
  84.9 85.2 %gather.1 = (bf16[2,640,3328]{2,1,0:T(8,128)(2,1)S(1)}, bf16[2,3200,640]{2,1,0:T(8,128)(2,1)S(1)}, bf16[2,4,640,768]{3,2,1,0:T(8,128)(2,1)S(1)}) custom-call(bf16[2,8,3328]{2,1,0:T(8,128)(2,1)S(1)} %fusion.17.w_a, bf16[2,32,640]{2,1,0:T(8,128)(2,1)S(1)} %pad.13.w_b, bf16[2,8,3072]{2,1,0:T(8,128)(2,1)S(1)} %pad.14.w_c), custom_call_target="tpu_custom_call" | custom-call | tf_op jit(solution)/shard_map/gather/pallas_call | solution.py:476
  170.2 8.4 %write.1 = (bf16[2,640,3200]{2,1,0:T(8,128)(2,1)}, bf16[2,640,3200]{2,1,0:T(8,128)(2,1)}, bf16[2,3200,640]{2,1,0:T(8,128)(2,1)}) custom-call(bf16[2,640,3328]{2,1,0:T(8,128)(2,1)S(1)} %get-tuple-element.21.a, bf16[2,3200,640]{2,1,0:T(8,128)(2,1)S(1)} %get-tuple-element.22.b, bf16[2,4,640,768]{3,2,1,0:T(8,128)(2,1)S(1)} %get-tuple-element.23.c), custom_call_target="tpu_custom_call" | custom-call | tf_op jit(solution)/shard_map/write/pallas_call | solution.py:494
  (5 shorter events, 0.1 us)
Async XLA Ops:
  0.6 77.4 %copy-start.4 = (f32[2,25,640]{2,0,1:T(2,128)S(1)}, f32[2,25,640]{2,0,1:T(2,128)}, u32[]{:S(2)}) copy-start(f32[2,25,640]{2,0,1:T(2,128)} %param.23) | copy-start | bytes 384004
  0.7 77.4 %copy-start.5 = (f32[2,25,640]{2,0,1:T(2,128)S(1)}, f32[2,25,640]{2,0,1:T(2,128)}, u32[]{:S(2)}) copy-start(f32[2,25,640]{2,0,1:T(2,128)} %param.20) | copy-start | bytes 384004
  0.7 80.0 %copy-start = (f32[2,5,3200]{2,0,1:T(2,128)S(1)}, f32[2,5,3200]{2,0,1:T(2,128)}, u32[]{:S(2)}) copy-start(f32[2,5,3200]{2,0,1:T(2,128)} %param.22) | copy-start | bytes 384004
  0.7 79.9 %copy-start.1 = (f32[2,5,3200]{2,0,1:T(2,128)S(1)}, f32[2,5,3200]{2,0,1:T(2,128)}, u32[]{:S(2)}) copy-start(f32[2,5,3200]{2,0,1:T(2,128)} %param.19) | copy-start | bytes 384004
  0.7 79.9 %copy-start.2 = (f32[2,5,3200]{2,0,1:T(2,128)S(1)}, f32[2,5,3200]{2,0,1:T(2,128)}, u32[]{:S(2)}) copy-start(f32[2,5,3200]{2,0,1:T(2,128)} %param.21) | copy-start | bytes 384004
  0.7 79.9 %copy-start.3 = (f32[2,5,3200]{2,0,1:T(2,128)S(1)}, f32[2,5,3200]{2,0,1:T(2,128)}, u32[]{:S(2)}) copy-start(f32[2,5,3200]{2,0,1:T(2,128)} %param.18) | copy-start | bytes 384004

commit v2 on v0

v2 whole, which is shorter than its diff:
```python
import jax
import jax.numpy as jnp
from jax import lax
from jax.experimental import pallas as pl
from jax.experimental.pallas import tpu as pltpu
from jax.sharding import PartitionSpec as P

ALL = slice(None)
BF, F32 = jnp.bfloat16, jnp.float32
D, FF, LANES, GROUP, OTHERS = 640, 3200, 128, 8, 7
OWN_A, OWN_B = 5, 25
BLOCK, SLAB, TALL, TALL4 = 40, 160, 200, 800
BLOCK_PAD, TALL_PAD = 48, 208
WIN, EDGE = 768, 3072
SHARE = 1
UC = 128 * SHARE
UA = 3200 - 4 * UC
WA = UA + 128
WC = 768 + UC
PLAN = "cab" * 10 + "pppppppppppppp" + "cab" * 6
PLAN += "cabcab" + "abc" + "a" + "ccc" + "b" + "aA" + "c" + "b" + "cc" + "B" + "c" + "Cab" + "ab" + "c" + "ABC" + "abc" + "ABC" + "abc" + "ABC"
PLAN += "f" * 7
SEND, RECV, LOCAL = 26, 142, 34
OFF = (2, 3, 1, 0)
HBM = pltpu.MemorySpace.HBM
VMEM = pltpu.MemorySpace.VMEM


def adamw(w, m, v, g):
    m = 0.9 * m + 0.1 * g
    v = 0.95 * v + 0.05 * g * g
    step = m * lax.rsqrt(v + 1e-8) + 0.1 * w
    return (w - 0.02 * step).astype(jnp.bfloat16), m, v


class Place:
    def __init__(self):
        me = lax.axis_index("dp")
        self.c = lax.rem(me, 2)
        self.z = lax.rem(me // 2, 4)
        self.y = lax.rem(me // GROUP, 4)
        self.x = me // 32
        self.g = lax.rem(me, GROUP)
        self.partner = self.dev(c=1 - self.c)

    def dev(self, x=None, y=None, z=None, c=None):
        x = self.x if x is None else x
        y = self.y if y is None else y
        z = self.z if z is None else z
        c = self.c if c is None else c
        return {"dp": ((x * 4 + y) * 4 + z) * 2 + c}

    def step(self, dim, by):
        return self.dev(**{dim: lax.rem(getattr(self, dim) + by, 4)})

    def group(self):
        out = [(self.z, 1 - self.c)]
        for dz in (1, 2, 3):
            zz = lax.rem(self.z + dz, 4)
            out += [(zz, self.c), (zz, 1 - self.c)]
        return out

    def barrier(self):
        sem = pltpu.get_barrier_semaphore()
        peers = [self.dev(z=z, c=c) for z, c in self.group()]
        peers += [self.step(d, by) for d in ("x", "y") for by in (1, 3)]
        for peer in peers:
            pl.semaphore_signal(sem, inc=1, device_id=peer, device_id_type=pl.DeviceIdType.MESH)
        pl.semaphore_wait(sem, len(peers))


class Sender:
    def __init__(self, send, recv):
        self.send, self.recv, self.n, self.groups, self.shared = send, recv, 0, {}, {}

    def start(self, src, dst, device, group, together=None):
        mine = self.groups.setdefault(group, len(self.groups))
        if together is None or together not in self.shared:
            got = self.n
            self.n += 1
            if together is not None:
                self.shared[together] = got
        else:
            got = self.shared[together]
        copy = pltpu.make_async_remote_copy(
            src_ref=src,
            dst_ref=dst,
            send_sem=self.send.at[mine],
            recv_sem=self.recv.at[got],
            device_id=device,
            device_id_type=pl.DeviceIdType.MESH,
        )
        copy.start()
        return copy

    def arrived(self, together, like):
        pltpu.make_async_copy(like, like, self.recv.at[self.shared[together]]).wait()

    def drain(self, sizes):
        for group, n in self.groups.items():
            like = sizes[group]
            pltpu.make_async_copy(like, like, self.send.at[n]).wait()


def rows(start, n):
    return pl.ds(pl.multiple_of(start, GROUP), n)


def total(refs, sl):
    acc = refs[0][sl].astype(F32)
    for r in refs[1:]:
        acc = acc + r[sl].astype(F32)
    return acc


def vadd(dst, refs, n, step):
    def body(i, carry):
        sl = (rows(i * step, step), ALL)
        dst[sl] = total(refs, sl).astype(dst.dtype)
        return carry

    lax.fori_loop(0, n // step, body, 0)


def interleave(plan, release, **programs):
    live = dict(programs)

    def advance(n):
        try:
            next(live[n])
        except StopIteration:
            del live[n]

    for n in plan:
        if n in release:
            release[n]()
        elif n in live:
            advance(n)
    while live:
        for n in list(live):
            advance(n)


def step_kernel(g_gate, g_up, g_down, w_gate, w_up, w_down, m_gate, m_up, m_down, v_gate, v_up, v_down,
                o_a, o_b, o_c, om_gate, om_up, om_down, ov_gate, ov_up, ov_down,
                own_a, own_b, own_c, ra, rb, rc, s1a, s2a, s1b, s2b, s1c, s2c, t1c, t2c, f_a, f_b, f_c,
                snd_a, snd_b, snd_c, rcv_a, rcv_b, rcv_c, new_a, new_b, new_c, got_a, got_b, got_c,
                wb_gate, wb_up, wb_down, fw_wide, fw_tall, w2_gate, w2_up, w2_down, m2_gate, m2_up, m2_down, v2_gate, v2_up, v2_down,
                send, recv, local):
    at = Place()
    x, y, z, c = at.x, at.y, at.z, at.c
    net = Sender(send, recv)
    loads = [0]
    rel = lambda base, j: lax.rem(base + OFF[j], 4)
    cols = lambda start, n: pl.ds(pl.multiple_of(start, LANES), n)

    def item_a(ref, k, j):
        return ref.at[rows(SLAB * k + BLOCK * rel(y, j), BLOCK), :]

    def item_b(ref, k, j):
        return ref.at[rows(TALL * k + TALL4 * rel(x, j), TALL), :]

    def item_c(ref, k, j):
        return ref.at[k, rows(SLAB * rel(x, j), SLAB), :]

    def moves_a(layer, ref, k, j):
        sl = rows(SLAB * k + BLOCK * rel(y, j), BLOCK)
        return [(g_up.at[0, layer, sl, pl.ds(0, UA)], ref.at[sl, pl.ds(0, UA)])]

    def moves_b(layer, ref, k, j):
        return [(g_down.at[0, layer, rows(TALL * k + TALL4 * rel(x, j), TALL), :], item_b(ref, k, j))]

    def moves_c(layer, ref, k, j):
        sl = rows(SLAB * rel(x, j), SLAB)
        out = [(g_gate.at[0, layer, sl, cols(WIN * k, WIN)], ref.at[k, sl, pl.ds(0, WIN)])]
        if UC:
            out.append((g_up.at[0, layer, sl, cols(UA + UC * k, UC)], ref.at[k, sl, pl.ds(WIN, UC)]))
        return out

    par_a, par_b, par_c = o_a.at[1 - c], o_b.at[1 - c], o_c.at[1 - c]
    there = {"a": o_a.at[c], "b": o_b.at[c], "c": o_c.at[c]}
    colours = {
        "c": (own_c, par_c, item_c, moves_c, z, "z", rc, SLAB, 32),
        "a": (own_a, par_a, item_a, moves_a, x, "x", ra, BLOCK, GROUP),
        "b": (own_b, par_b, item_b, moves_b, y, "y", rb, TALL, BLOCK),
    }

    locals_ = {}

    def load(src, dst, together):
        n = locals_.setdefault(together, len(locals_))
        pltpu.make_async_copy(src, dst, local.at[n]).start()

    def loaded(together, like):
        pltpu.make_async_copy(like, like, local.at[locals_[together]]).wait()

    sets = (((2, 0),), ((2, 2),), ((1, 2), (3, 0)), ((1, 0), (3, 2)), ((2, 1), (2, 3)), ((1, 3), (3, 1)), ((0, 0), (0, 2)), ((1, 1), (3, 3), (0, 1), (0, 3)))
    tail = (ALL, pl.ds(EDGE, LANES)), (ALL, pl.ds(UA, LANES))
    wide, tall = rows(SLAB * x + BLOCK * y, BLOCK), rows(TALL4 * x + TALL * y, TALL)
    state = [(w_gate.at[:, wide, :], wb_gate), (w_up.at[:, wide, :], wb_up), (w_down.at[:, tall, :], wb_down)]
    moments = ((m_gate, om_gate, m2_gate), (m_up, om_up, m2_up), (m_down, om_down, m2_down),
               (v_gate, ov_gate, v2_gate), (v_up, ov_up, v2_up), (v_down, ov_down, v2_down))
    state += [(src, dst) for src, dst, _ in moments]
    load(g_gate.at[(0, c, *tail[0])], own_a.at[tail[1]], "tail")
    for i, part in enumerate(sets):
        for dk, j in part:
            for n, (own, par, item, moves, k0, *_) in colours.items():
                for src, dst in moves(c, own, lax.rem(k0 + dk, 4), j):
                    load(src, dst, (n, i))
    for i, (src, dst) in enumerate(state):
        load(src, dst, ("state", i))
    at.barrier()
    net.start(g_gate.at[(0, 1 - c, *tail[0])], there["a"].at[tail[1]], at.partner, "da", "tail")
    for i, part in enumerate(sets):
        for dk, j in part:
            for n, (own, par, item, moves, k0, *_) in colours.items():
                for src, dst in moves(1 - c, there[n], lax.rem(k0 + dk, 4), j):
                    net.start(src, dst, at.partner, "d" + n, (n, i))
    here_is = set()

    def here_now(n, dk, j):
        i = [i for i, part in enumerate(sets) if (dk, j) in part][0]
        if (n, i) in here_is:
            return
        here_is.add((n, i))
        count = len(sets[i])
        if n == "a":
            like = own_a.at[pl.ds(0, BLOCK * count), pl.ds(0, UA)]
        elif n == "b":
            like = own_b.at[pl.ds(0, TALL * count), :]
        else:
            like = own_c.at[0, pl.ds(0, SLAB * count), :]
        loaded((n, i), like)
        net.arrived((n, i), like)

    def first(n):
        own, par, item, moves, k0, dim, r, height, step = colours[n]
        up, down = at.step(dim, 1), at.step(dim, 3)
        k2, kp, km = (lax.rem(k0 + d, 4) for d in (2, 1, 3))
        one, two = {}, {}
        if n == "a":
            like = own_a.at[:, pl.ds(0, LANES)]
            loaded("tail", like)
            net.arrived("tail", like)

        def opposite(j):
            here_now(n, 2, j)
            here = item(own, k2, j)
            vadd(here, (here, item(par, k2, j)), height, step)
            one[j] = net.start(here, r.at[j], up if j < 2 else down, "f" + n)

        def beside(dk, j, more):
            here_now(n, dk, j)
            if more:
                one[j].wait_recv()
            here = item(own, kp if dk == 1 else km, j)
            par_here = item(par, kp if dk == 1 else km, j)
            vadd(here, (here, par_here, r.at[j]) if more else (here, par_here), height, step)
            two[dk, j] = net.start(here, r.at[4 + j if dk == 1 else GROUP + j], up if dk == 1 else down, "f" + n)

        def mine(j):
            here_now(n, 0, j)
            two[1, j].wait_recv()
            two[3, j].wait_recv()
            here = item(own, k0, j)
            vadd(here, (here, item(par, k0, j), r.at[4 + j], r.at[GROUP + j]), height, step)

        opposite(0)
        yield
        opposite(2)
        yield
        beside(1, 2, False)
        yield
        beside(3, 0, False)
        yield
        beside(1, 0, True)
        yield
        beside(3, 2, True)
        yield
        opposite(1)
        yield
        opposite(3)
        yield
        beside(1, 3, False)
        yield
        beside(3, 1, False)
        yield
        mine(0)
        yield 0
        mine(2)
        yield 2
        beside(1, 1, True)
        yield
        beside(3, 3, True)
        yield
        mine(1)
        yield 1
        mine(3)
        yield 3

    def later(n, dim, block, halves, r1, r2, ready, step, done):
        up, down = at.step(dim, 1), at.step(dim, 3)
        for j in ready or (0, 2, 1, 3):
            if j == 0:
                a = net.start(halves(block(0), 0), halves(r1.at[0], 0, True), up, n)
                b = net.start(halves(block(0), 1), halves(r1.at[1], 1, True), down, n)
            if j == 2:
                net.start(halves(block(2), 1), halves(r2.at[0], 1), up, n, n)
            if j == 1:
                net.start(halves(block(1), 0), halves(r2.at[1], 0), down, n, n)
            if ready:
                yield
        a.wait_recv()
        here = halves(block(2), 0)
        vadd(here, (here, halves(r1.at[0], 0, True)), here.shape[0], GROUP)
        net.start(here, halves(r2.at[0], 0), up, n, n)
        yield
        b.wait_recv()
        here = halves(block(1), 1)
        vadd(here, (here, halves(r1.at[1], 1, True)), here.shape[0], GROUP)
        net.start(here, halves(r2.at[1], 1), down, n, n)
        yield
        net.arrived(n, r2)
        vadd(done, (block(3), r2.at[0], r2.at[1]), block(3).shape[0], step)

    def by_cols(w):
        def cut(ref, h, packed=False):
            return ref if packed else ref.at[:, pl.ds(h * w, w)]

        return cut

    def by_rows(n0, n1):
        def cut(ref, h, packed=False):
            return ref.at[pl.ds(0, (n0, n1)[h]), :] if packed else ref.at[pl.ds((0, n0)[h], (n0, n1)[h]), :]

        return cut

    def spread(n, full, blocks, height, snd, rcv):
        for k in range(GROUP):
            snd[k] = full[pl.ds(blocks * k, height), :].astype(BF)
        for zz, cc in at.group():
            s = 2 * zz + cc
            net.start(snd.at[s], rcv.at[at.g], at.dev(z=zz, c=cc), "s" + n, "s" + n)
        rcv[at.g] = snd[at.g]

    def prepare():
        for ref in (w2_gate, w2_up, w2_down, m2_gate, m2_up, m2_down, v2_gate, v2_up, v2_down):
            ref[...] = jnp.zeros(ref.shape, F32)
        for i, (_, dst) in enumerate(state):
            loaded(("state", i), dst)
        yield
        fw_wide[pl.ds(BLOCK, GROUP), :] = jnp.zeros((GROUP, FF), F32)
        fw_tall[pl.ds(TALL, GROUP), :] = jnp.zeros((GROUP, D), F32)
        for block, full, out, n, height in ((wb_gate, fw_wide, w2_gate, OWN_A, GROUP), (wb_up, fw_wide, w2_up, OWN_A, GROUP), (wb_down, fw_tall, w2_down, OWN_B, 32)):
            for layer in range(2):
                full[pl.ds(0, GROUP * n), :] = block[layer].astype(F32)
                for k in range(GROUP):

                    @pl.when(at.g == k)
                    def _():
                        out[layer] = full[pl.ds(n * k, height), :]

                yield
        for _, src, out in moments:
            for r in range(src.shape[0]):
                for layer in range(2):
                    out[layer, pl.ds(r, 1), :] = src[r, pl.ds(layer, 1), :]
            yield

    updated = []

    def finish():
        assert len(updated) == 3
        for _, out, src in moments:
            for r in range(out.shape[0]):
                for layer in range(2):
                    out[r, pl.ds(layer, 1), :] = src[layer, pl.ds(r, 1), :]
            yield

    gate, up_, down_ = (w2_gate, m2_gate, v2_gate), (w2_up, m2_up, v2_up), (w2_down, m2_down, v2_down)

    def update(which, start, layer, g, new, at_col):
        sl = (layer, ALL, pl.ds(start, g.shape[1]))
        w2, m2, v2 = which
        new_w, m2[sl], v2[sl] = adamw(w2[sl], m2[sl], v2[sl], g)
        new[layer, :, pl.ds(at_col, g.shape[1])] = new_w

    def summed(rcv, layer, sl):
        acc = rcv[layer, :, sl].astype(F32)
        for zz in range(1, 4):
            acc = acc + rcv[2 * zz + layer, :, sl].astype(F32)
        return acc.astype(BF).astype(F32)

    def pieces(start, end, most=896):
        return [(i, min(most, end - i)) for i in range(start, end, most)]

    def step_a():
        for layer in range(2):
            for i, n in pieces(0, UA):
                update(up_, i, layer, summed(rcv_a, layer, pl.ds(i, n)), new_a, i)
            update(gate, EDGE, layer, summed(rcv_a, layer, pl.ds(UA, LANES)), new_a, UA)

    def step_b():
        for layer in range(2):
            update(down_, 0, layer, summed(rcv_b, layer, pl.ds(0, D)), new_b, 0)

    def step_c():
        for layer in range(2):
            for zz in range(4):
                g = rcv_c[2 * zz + layer].astype(F32)
                update(gate, WIN * zz, layer, g[:, :WIN], new_c, WC * zz)
                if UC:
                    update(up_, UA + UC * zz, layer, g[:, WIN:], new_c, WC * zz + WIN)


    def over(n, ref):
        net.start(ref, ref, at.partner, "x" + n, "x" + n)

    def share(n, new, got):
        sl = (ALL, cols(WC * z, WC)) if n == "c" else (ALL, ALL)
        for zz, cc in at.group():
            there = (ALL, cols(WC * zz, WC)) if n == "c" else sl
            net.start(new.at[(cc, *there)], got.at[at.g], at.dev(z=zz, c=cc), "w" + n, "w" + n)
        got[at.g] = new[(c, *sl)]

    def build(n, blocks, got, full, out):
        net.arrived("w" + n, got.at[pl.ds(0, OTHERS)])
        for k in range(GROUP):
            full[pl.ds(blocks * k, blocks), :] = got[k].astype(F32)[:blocks]
        out[...] = full[pl.ds(0, GROUP * blocks), :].astype(BF)

    release = {}

    def small(n, dim, block, halves, brief=False):
        up, down = at.step(dim, 1), at.step(dim, 3)
        mine = block(3)
        m0 = net.start(halves(mine, 0), halves(mine, 0), up, n)
        p1 = net.start(halves(mine, 1), halves(mine, 1), down, n)
        m1 = net.start(halves(mine, 1), halves(mine, 1), up, n)
        p0 = net.start(halves(mine, 0), halves(mine, 0), down, n)
        yield 3
        m0.wait_recv()
        here = halves(block(1), 0)
        f0 = net.start(here, here, up, n)
        p1.wait_recv()
        here = halves(block(2), 1)
        f1 = net.start(here, here, down, n)
        yield
        m1.wait_recv()
        if not brief:
            yield 1
        p0.wait_recv()
        if not brief:
            yield 2
        f0.wait_recv()
        f1.wait_recv()
        if not brief:
            yield 0

    def large(n, dim, k0, item, ready):
        up, down = at.step(dim, 1), at.step(dim, 3)
        kp, km, k2 = (lax.rem(k0 + d, 4) for d in (1, 3, 2))
        fm, fp, order, held = {}, {}, [], []

        def flush():
            if held:
                j = held.pop(0)
                here = item(k0, j)
                fm[j] = net.start(here, here, up, "l" + n)
                fp[j] = net.start(here, here, down, "l" + n)
                over(n, here)
                order.append(j)

        release[n.upper()] = flush
        for j in ready:
            if j is not None:
                held.append(j)
            yield
        while held:
            flush()
            yield
        f2 = {}
        for j in order:
            fm[j].wait_recv()
            here = item(km, j)
            if j < 2:
                f2[j] = net.start(here, here, up, "l" + n)
            over(n, here)
            yield
            fp[j].wait_recv()
            here = item(kp, j)
            if j >= 2:
                f2[j] = net.start(here, here, down, "l" + n)
            over(n, here)
            yield
        for j in order:
            f2[j].wait_recv()
            over(n, item(k2, j))
            yield

    def colour_a():
        f_a[pl.ds(BLOCK, GROUP), :] = jnp.zeros((GROUP, WA), F32)
        yield from later("ma", "y", lambda j: item_a(own_a, x, j), by_cols(WA // 2), s1a, s2a, first("a"), GROUP, f_a)
        spread("a", f_a, OWN_A, GROUP, snd_a, rcv_a)
        yield
        net.arrived("sa", rcv_a.at[pl.ds(0, OTHERS)])
        step_a()
        updated.append("a")
        share("a", new_a, got_a)
        yield
        out = lambda k, j: item_a(o_a.at[c], k, j)
        build("a", OWN_A, got_a, f_a, out(x, 3))
        yield from large("a", "x", x, out, small("ga", "y", lambda j: out(x, j), by_cols(WA // 2)))

    def colour_b():
        f_b[pl.ds(TALL, GROUP), :] = jnp.zeros((GROUP, D), F32)
        yield from later("mb", "x", lambda j: item_b(own_b, y, j), by_rows(104, 96), s1b, s2b, first("b"), BLOCK, f_b)
        spread("b", f_b, OWN_B, 32, snd_b, rcv_b)
        yield
        net.arrived("sb", rcv_b.at[pl.ds(0, OTHERS)])
        step_b()
        updated.append("b")
        share("b", new_b, got_b)
        yield
        out = lambda k, j: item_b(o_b.at[c], k, j)
        build("b", OWN_B, got_b, f_b, out(y, 3))
        yield from large("b", "y", y, out, small("gb", "x", lambda j: out(y, j), by_rows(104, 96)))

    def colour_c():
        f_c[pl.ds(BLOCK, GROUP), :] = jnp.zeros((GROUP, WC), F32)
        yield from later("mc", "x", lambda j: item_c(own_c, z, j), by_rows(80, 80), s1c, s2c, first("c"), 32, item_c(own_c, z, 3))
        block = lambda j: own_c.at[z, rows(SLAB * x + BLOCK * rel(y, j), BLOCK), :]
        split = by_cols(WC // 2) if WC % 256 == 0 else by_rows(24, 16)
        yield from later("nc", "y", block, split, t1c, t2c, None, GROUP, f_c)
        spread("c", f_c, OWN_A, GROUP, snd_c, rcv_c)
        yield
        net.arrived("sc", rcv_c.at[pl.ds(0, OTHERS)])
        step_c()
        updated.append("c")
        share("c", new_c, got_c)
        yield
        out = lambda k, j: item_c(o_c.at[c], k, j)
        mine = lambda j: o_c.at[c, z, rows(SLAB * x + BLOCK * rel(y, j), BLOCK), :]
        build("c", OWN_A, got_c, f_c, mine(3))
        for _ in small("hc", "y", mine, split, True):
            yield
        yield from large("c", "z", z, out, small("gc", "x", lambda j: out(z, j), by_rows(80, 80)))

    interleave(PLAN, release, c=colour_c(), a=colour_a(), b=colour_b(), p=prepare(), f=finish())
    for n, (own, *_) in colours.items():
        net.arrived("x" + n, own)
    sizes = {"nc": own_c.at[0, pl.ds(0, 120), :], "hc": own_c.at[0, pl.ds(0, 120), :]}
    for n, (own, _, _, _, _, _, r, *_) in colours.items():
        sizes |= {"d" + n: own, "x" + n: own, "f" + n: r, "l" + n: r, "m" + n: r.at[pl.ds(0, 3)], "g" + n: r.at[pl.ds(0, 3)]}
    for n, rcv in (("a", rcv_a), ("b", rcv_b), ("c", rcv_c)):
        sizes |= {"s" + n: rcv.at[pl.ds(0, OTHERS)], "w" + n: rcv.at[pl.ds(0, OTHERS)]}
    net.drain(sizes)
    assert (net.n, len(net.groups), len(locals_)) == (RECV, SEND, LOCAL), (net.n, len(net.groups), len(locals_))


def write_kernel(a, b, c, *refs):
    small, (gate, up, down), outs, sem = refs[:6], refs[6:9], refs[9:15], refs[15]
    copies = [(b.at[l], down.at[l]) for l in range(2)]
    copies += [(a.at[l, :, pl.ds(0, UA)], up.at[l, :, pl.ds(0, UA)]) for l in range(2)]
    copies += [(c.at[l, k, :, pl.ds(0, WIN)], gate.at[l, :, pl.ds(WIN * k, WIN)]) for l in range(2) for k in range(4)]
    copies += [(a.at[l, :, pl.ds(UA, LANES)], gate.at[l, :, pl.ds(EDGE, LANES)]) for l in range(2)]
    if UC:
        copies += [(c.at[l, k, :, pl.ds(WIN, UC)], up.at[l, :, pl.ds(UA + UC * k, UC)]) for l in range(2) for k in range(4)]
    copies += list(zip(small, outs, strict=True))
    copies = [pltpu.make_async_copy(s, d, sem.at[i]) for i, (s, d) in enumerate(copies)]
    for copy in copies:
        copy.start()
    for copy in copies:
        copy.wait()


def spec(space, n):
    return [pl.BlockSpec(memory_space=space)] * n


def solution(mesh):
    def step(*arrays):
        terms, weights, m, v = (arrays[i : i + 3] for i in (0, 3, 6, 9))
        turn = lambda one: jnp.transpose(one, (1, 0, 2))
        moments = [turn(one) for one in (*m, *v)]
        own_rows = [(2, GROUP, FF), (2, GROUP, FF), (2, 32, D)]
        blocks = [(GROUP, GROUP, WA), (GROUP, 32, D), (GROUP, GROUP, WC)]
        results = pl.pallas_call(
            step_kernel,
            out_shape=[
                VMEM((2, D, WA), BF),
                VMEM((2, FF, D), BF),
                VMEM((2, 4, D, WC), BF),
                *[VMEM(one.shape, F32) for one in moments],
            ],
            in_specs=spec(HBM, 12),
            out_specs=spec(VMEM, 9),
            scratch_shapes=[
                VMEM((D, WA), BF),
                VMEM((FF, D), BF),
                VMEM((4, D, WC), BF),
                *[VMEM((12, *s), BF) for s in ((BLOCK, WA), (TALL, D), (SLAB, WC))],
                VMEM((2, BLOCK, WA // 2), BF),
                VMEM((2, BLOCK, WA), BF),
                VMEM((2, 104, D), BF),
                VMEM((2, TALL, D), BF),
                VMEM((2, 80, WC), BF),
                VMEM((2, SLAB, WC), BF),
                VMEM((2, BLOCK, WC // 2) if WC % 256 == 0 else (2, 24, WC), BF),
                VMEM((2, BLOCK, WC), BF),
                VMEM((BLOCK_PAD, WA), F32),
                VMEM((TALL_PAD, D), F32),
                VMEM((BLOCK_PAD, WC), F32),
                *[VMEM(s, BF) for s in blocks] * 2,
                VMEM((2, GROUP, WA), BF),
                VMEM((2, 32, D), BF),
                VMEM((2, GROUP, 4 * WC), BF),
                *[VMEM(s, BF) for s in blocks],
                VMEM((2, BLOCK, FF), BF),
                VMEM((2, BLOCK, FF), BF),
                VMEM((2, TALL, D), BF),
                VMEM((BLOCK_PAD, FF), F32),
                VMEM((TALL_PAD, D), F32),
                *[VMEM(s, F32) for s in own_rows] * 3,
                pltpu.SemaphoreType.DMA((SEND,)),
                pltpu.SemaphoreType.DMA((RECV,)),
                pltpu.SemaphoreType.DMA((LOCAL,)),
            ],
            compiler_params=pltpu.CompilerParams(collective_id=0, has_side_effects=True, vmem_limit_bytes=34 * 2**20),
            name="step",
        )(*terms, *weights, *moments)
        done = pl.pallas_call(
            write_kernel,
            out_shape=[jax.ShapeDtypeStruct(w.shape, BF) for w in weights] + [jax.ShapeDtypeStruct(one.shape, F32) for one in moments],
            in_specs=spec(VMEM, 9),
            out_specs=spec(HBM, 9),
            scratch_shapes=[pltpu.SemaphoreType.DMA((30,))],
            compiler_params=pltpu.CompilerParams(vmem_limit_bytes=2**20),
            name="write",
        )(*results)
        return (*done[:3], *(turn(one) for one in done[3:]))

    all_of, cut = P(None, None, None), P(None, "dp", None)
    return jax.shard_map(
        step,
        mesh=mesh,
        in_specs=(P(("rep", "dp"), None, None, None),) * 3 + (all_of,) * 3 + (cut,) * 6,
        out_specs=(P("rep", None, None),) * 3 + (P("rep", "dp", None),) * 6,
        check_vma=False,
    )
```

time: 544 us -> 147 us (0.27)
  waiting for transfers between devices: 420 us -> 0 us
  Pallas kernels: 0 us -> 146 us
  local copies, waits for them, and re-layouts: 104 us -> 0 us
  between operations: 13.9 us -> 0.65 us
  other arithmetic: 5.64 us -> 0 us
    unnamed x5 -> x0, waiting for transfers between devices: 230 us -> none
    all_gather x3 -> x0, waiting for transfers between devices: 190 us -> none  [step(): whole = [lax.all_gather(one[0], 'dp', axis=1, tiled=True) for one in new]]
    pallas_call x0 -> x2, Pallas kernels: none -> 146 us  [the longest x1 137 us: step(): pl.pallas_call(step_kernel, out_shape=[VMEM((2, D, WA), BF), VMEM((2, FF,...]
    unnamed x20 -> x0, local copies, waits for them, and re-layouts: 61.5 us -> none
    squeeze x1 -> x0, local copies, waits for them, and re-layouts: 40 us -> none  [step(): t[0]]
    convert_element_type x3 -> x0, other arithmetic: 5.64 us -> none  [adamw(): return ((w - 0.02 * step).astype(jnp.bfloat16), m, v)]
  transfers between devices with their start and end apart: 4 -> 0, of which waited for: 4 -> 0; matrix products, arithmetic and copies ran while one was open for 4% -> 0% of each run, Pallas kernels for 0% -> 0%
where the time goes in v2:
time: 147 us; the launch traced here: 146 us
  Pallas kernels  146 us (99%)
    pallas_call x1, Pallas kernels, step(): pl.pallas_call(step_kernel, out_shape=[VMEM((2, D, WA), BF), VMEM((2, FF,...  137 us
    pallas_call x1, Pallas kernels, step(): pl.pallas_call(write_kernel, out_shape=[jax.ShapeDtypeStruct(w.shape, BF)...  8.74 us

profile of v2, /device:TPU:1, one launch (start us, length us, event | category | flops | bytes accessed | tf_op | source)
XLA Modules:
  0.0 146.5 jit_solution(10521594524924711963)
XLA Ops:
  0.6 137.1 %step.1 = (bf16[2,640,2816]{2,1,0:T(8,128)(2,1)S(1)}, bf16[2,3200,640]{2,1,0:T(8,128)(2,1)S(1)}, bf16[2,4,640,896]{3,2,1,0:T(8,128)(2,1)S(1)}, f32[5,2,3200]{2,1...) custom-call(bf16[1,2,640,3200]{3,2,1,0:T(8,128)(2,1)} %g_gate.1, ...), custom_call_target="tpu_custom_call" | custom-call | tf_op jit(solution)/shard_map/step/pallas_call | solution.py:588
  137.7 8.7 %write.1 = (bf16[2,640,3200]{2,1,0:T(8,128)(2,1)}, bf16[2,640,3200]{2,1,0:T(8,128)(2,1)}, bf16[2,3200,640]{2,1,0:T(8,128)(2,1)}, f32[5,2,3200]{2,1,0:T(2,128)}, ...) custom-call(bf16[2,640,2816]{2,1,0:T(8,128)(2,1)S(1)} %get-tuple-ele, ...), custom_call_target="tpu_custom_call" | custom-call | tf_op jit(solution)/shard_map/write/pallas_call | solution.py:632

commit v3 on v2

--- a/solution.py
+++ b/solution.py
@@ -17,10 +17,11 @@
 UA = 3200 - 4 * UC
 WA = UA + 128
 WC = 768 + UC
-PLAN = "cab" * 10 + "pppppppppppppp" + "cab" * 6
-PLAN += "cabcab" + "abc" + "a" + "ccc" + "b" + "aA" + "c" + "b" + "cc" + "B" + "c" + "Cab" + "ab" + "c" + "ABC" + "abc" + "ABC" + "abc" + "ABC"
-PLAN += "f" * 7
-SEND, RECV, LOCAL = 26, 142, 34
+PACK_A, PACK_B, PACK_C = 112, 128, 40
+PLAN = "cab" * 10 + "pppppppp" + "cab" * 2 + "pppppppppp" + "acb" * 2 + "aaaa" + "cbcb" + "cbcb"
+PLAN += "aacb" + "aA" + "cb" + "cb" + "cc" + "C" + "abB" + "abc" + "ABC" + "abc" + "ABC" + "abc" + "ABC"
+PLAN += "f" * 9
+SEND, RECV, LOCAL = 26, 120, 34
 OFF = (2, 3, 1, 0)
 HBM = pltpu.MemorySpace.HBM
 VMEM = pltpu.MemorySpace.VMEM
@@ -143,9 +144,9 @@
 
 def step_kernel(g_gate, g_up, g_down, w_gate, w_up, w_down, m_gate, m_up, m_down, v_gate, v_up, v_down,
                 o_a, o_b, o_c, om_gate, om_up, om_down, ov_gate, ov_up, ov_down,
-                own_a, own_b, own_c, ra, rb, rc, s1a, s2a, s1b, s2b, s1c, s2c, t1c, t2c, f_a, f_b, f_c,
+                own_a, own_b, own_c, ra, rb, rc, s1a, s2a, s1b, s2b, s1c, s2c, tc, f_a, f_b, f_c,
                 snd_a, snd_b, snd_c, rcv_a, rcv_b, rcv_c, new_a, new_b, new_c, got_a, got_b, got_c,
-                wb_gate, wb_up, wb_down, fw_wide, fw_tall, w2_gate, w2_up, w2_down, m2_gate, m2_up, m2_down, v2_gate, v2_up, v2_down,
+                wb_gate, wb_up, wb_down, fw_wide, fw_tall, pk_a, pk_b, pk_c, sw_a, sw_b, sw_c, sm_a, sm_b, sm_c, sv_a, sv_b, sv_c, w2_gate, w2_up, w2_down, m2_gate, m2_up, m2_down, v2_gate, v2_up, v2_down,
                 send, recv, local):
     at = Place()
     x, y, z, c = at.x, at.y, at.z, at.c
@@ -237,7 +238,7 @@
         own, par, item, moves, k0, dim, r, height, step = colours[n]
         up, down = at.step(dim, 1), at.step(dim, 3)
         k2, kp, km = (lax.rem(k0 + d, 4) for d in (2, 1, 3))
-        one, two = {}, {}
+        one = {}
         if n == "a":
             like = own_a.at[:, pl.ds(0, LANES)]
             loaded("tail", like)
@@ -256,12 +257,11 @@
             here = item(own, kp if dk == 1 else km, j)
             par_here = item(par, kp if dk == 1 else km, j)
             vadd(here, (here, par_here, r.at[j]) if more else (here, par_here), height, step)
-            two[dk, j] = net.start(here, r.at[4 + j if dk == 1 else GROUP + j], up if dk == 1 else down, "f" + n)
+            net.start(here, r.at[4 + j if dk == 1 else GROUP + j], up if dk == 1 else down, "f" + n, (n, "two", j))
 
         def mine(j):
             here_now(n, 0, j)
-            two[1, j].wait_recv()
-            two[3, j].wait_recv()
+            net.arrived((n, "two", j), r.at[pl.ds(0, 2)])
             here = item(own, k0, j)
             vadd(here, (here, item(par, k0, j), r.at[4 + j], r.at[GROUP + j]), height, step)
 
@@ -298,18 +298,22 @@
         mine(3)
         yield 3
 
-    def later(n, dim, block, halves, r1, r2, ready, step, done):
+    def later(n, dim, block, halves, r1, r2, ready, hold, step, done):
         up, down = at.step(dim, 1), at.step(dim, 3)
-        for j in ready or (0, 2, 1, 3):
-            if j == 0:
-                a = net.start(halves(block(0), 0), halves(r1.at[0], 0, True), up, n)
-                b = net.start(halves(block(0), 1), halves(r1.at[1], 1, True), down, n)
-            if j == 2:
-                net.start(halves(block(2), 1), halves(r2.at[0], 1), up, n, n)
-            if j == 1:
-                net.start(halves(block(1), 0), halves(r2.at[1], 0), down, n, n)
-            if ready:
-                yield
+        waiting = []
+        for i, chunk in enumerate(ready):
+            if chunk is not None:
+                waiting.append(chunk)
+            while waiting and i >= hold:
+                j = waiting.pop(0)
+                if j == 0:
+                    a = net.start(halves(block(0), 0), halves(r1.at[0], 0, True), up, n)
+                    b = net.start(halves(block(0), 1), halves(r1.at[1], 1, True), down, n)
+                if j == 2:
+                    net.start(halves(block(2), 1), halves(r2.at[0], 1), up, n, n)
+                if j == 1:
+                    net.start(halves(block(1), 0), halves(r2.at[1], 0), down, n, n)
+            yield
         a.wait_recv()
         here = halves(block(2), 0)
         vadd(here, (here, halves(r1.at[0], 0, True)), here.shape[0], GROUP)
@@ -335,16 +339,18 @@
 
         return cut
 
-    def spread(n, full, blocks, height, snd, rcv):
+    def spread(n, full, blocks, packed, snd, rcv):
         for k in range(GROUP):
-            snd[k] = full[pl.ds(blocks * k, height), :].astype(BF)
+            for t in range(full.shape[1] // LANES):
+                packed[k, pl.ds(blocks * t, blocks), :] = full[pl.ds(blocks * k, blocks), pl.ds(LANES * t, LANES)]
+            snd[k] = packed[k].astype(BF)
         for zz, cc in at.group():
             s = 2 * zz + cc
             net.start(snd.at[s], rcv.at[at.g], at.dev(z=zz, c=cc), "s" + n, "s" + n)
         rcv[at.g] = snd[at.g]
 
     def prepare():
-        for ref in (w2_gate, w2_up, w2_down, m2_gate, m2_up, m2_down, v2_gate, v2_up, v2_down):
+        for ref in (sw_a, sw_b, sw_c, sm_a, sm_b, sm_c, sv_a, sv_b, sv_c):
             ref[...] = jnp.zeros(ref.shape, F32)
         for i, (_, dst) in enumerate(state):
             loaded(("state", i), dst)
@@ -366,72 +372,88 @@
                 for layer in range(2):
                     out[layer, pl.ds(r, 1), :] = src[r, pl.ds(layer, 1), :]
             yield
-
+        for which in kept:
+            for to, here, there in tiles(*which):
+                here[to] = there[...]
+            yield
+
+    def tiles(wide_gate, wide_up, tall, in_a, in_b, in_c):
+        for layer in range(2):
+            for t in range(OWN_B):
+                piece = (layer, pl.ds(0, OWN_A), pl.ds(LANES * t, LANES))
+                if t < 24:
+                    yield (layer, t // 6, pl.ds(OWN_A * (t % 6), OWN_A)), in_c, wide_gate.at[piece]
+                else:
+                    yield (layer, pl.ds(OWN_A * (UA // LANES), OWN_A)), in_a, wide_gate.at[piece]
+                if t < UA // LANES:
+                    yield (layer, pl.ds(OWN_A * t, OWN_A)), in_a, wide_up.at[piece]
+                else:
+                    yield (layer, (t - UA // LANES) // SHARE, pl.ds(OWN_A * (6 + (t - UA // LANES) % SHARE), OWN_A)), in_c, wide_up.at[piece]
+            for t in range(OWN_A):
+                yield (layer, pl.ds(OWN_B * t, OWN_B)), in_b, tall.at[layer, pl.ds(0, OWN_B), pl.ds(LANES * t, LANES)]
+
+    kept = (
+        (w2_gate, w2_up, w2_down, sw_a, sw_b, sw_c),
+        (m2_gate, m2_up, m2_down, sm_a, sm_b, sm_c),
+        (v2_gate, v2_up, v2_down, sv_a, sv_b, sv_c),
+    )
     updated = []
 
     def finish():
         assert len(updated) == 3
+        for which in kept[1:]:
+            for to, here, there in tiles(*which):
+                there[...] = here[to]
+            yield
         for _, out, src in moments:
             for r in range(out.shape[0]):
                 for layer in range(2):
                     out[r, pl.ds(layer, 1), :] = src[layer, pl.ds(r, 1), :]
             yield
 
-    gate, up_, down_ = (w2_gate, m2_gate, v2_gate), (w2_up, m2_up, v2_up), (w2_down, m2_down, v2_down)
-
-    def update(which, start, layer, g, new, at_col):
-        sl = (layer, ALL, pl.ds(start, g.shape[1]))
-        w2, m2, v2 = which
-        new_w, m2[sl], v2[sl] = adamw(w2[sl], m2[sl], v2[sl], g)
-        new[layer, :, pl.ds(at_col, g.shape[1])] = new_w
-
-    def summed(rcv, layer, sl):
-        acc = rcv[layer, :, sl].astype(F32)
+    def update(state, at_, g, new):
+        w2, m2, v2 = state
+        new[at_], m2[at_], v2[at_] = adamw(w2[at_], m2[at_], v2[at_], g)
+
+    def summed(rcv, layer):
+        acc = rcv[layer].astype(F32)
         for zz in range(1, 4):
-            acc = acc + rcv[2 * zz + layer, :, sl].astype(F32)
+            acc = acc + rcv[2 * zz + layer].astype(F32)
         return acc.astype(BF).astype(F32)
-
-    def pieces(start, end, most=896):
-        return [(i, min(most, end - i)) for i in range(start, end, most)]
 
     def step_a():
         for layer in range(2):
-            for i, n in pieces(0, UA):
-                update(up_, i, layer, summed(rcv_a, layer, pl.ds(i, n)), new_a, i)
-            update(gate, EDGE, layer, summed(rcv_a, layer, pl.ds(UA, LANES)), new_a, UA)
+            update((sw_a, sm_a, sv_a), layer, summed(rcv_a, layer), new_a)
 
     def step_b():
         for layer in range(2):
-            update(down_, 0, layer, summed(rcv_b, layer, pl.ds(0, D)), new_b, 0)
+            update((sw_b, sm_b, sv_b), layer, summed(rcv_b, layer), new_b)
 
     def step_c():
         for layer in range(2):
             for zz in range(4):
-                g = rcv_c[2 * zz + layer].astype(F32)
-                update(gate, WIN * zz, layer, g[:, :WIN], new_c, WC * zz)
-                if UC:
-                    update(up_, UA + UC * zz, layer, g[:, WIN:], new_c, WC * zz + WIN)
-
+                update((sw_c, sm_c, sv_c), (layer, zz), rcv_c[2 * zz + layer].astype(F32), new_c)
 
     def over(n, ref):
         net.start(ref, ref, at.partner, "x" + n, "x" + n)
 
     def share(n, new, got):
-        sl = (ALL, cols(WC * z, WC)) if n == "c" else (ALL, ALL)
         for zz, cc in at.group():
-            there = (ALL, cols(WC * zz, WC)) if n == "c" else sl
-            net.start(new.at[(cc, *there)], got.at[at.g], at.dev(z=zz, c=cc), "w" + n, "w" + n)
-        got[at.g] = new[(c, *sl)]
+            one = new.at[cc, zz] if n == "c" else new.at[cc]
+            net.start(one, got.at[at.g], at.dev(z=zz, c=cc), "w" + n, "w" + n)
+        got[at.g] = new[c, z] if n == "c" else new[c]
 
     def build(n, blocks, got, full, out):
         net.arrived("w" + n, got.at[pl.ds(0, OTHERS)])
         for k in range(GROUP):
-            full[pl.ds(blocks * k, blocks), :] = got[k].astype(F32)[:blocks]
+            one = got[k].astype(F32)
+            for t in range(full.shape[1] // LANES):
+                full[pl.ds(blocks * k, blocks), pl.ds(LANES * t, LANES)] = one[blocks * t : blocks * (t + 1)]
         out[...] = full[pl.ds(0, GROUP * blocks), :].astype(BF)
 
     release = {}
 
-    def small(n, dim, block, halves, brief=False):
+    def small(n, dim, block, halves):
         up, down = at.step(dim, 1), at.step(dim, 3)
         mine = block(3)
         m0 = net.start(halves(mine, 0), halves(mine, 0), up, n)
@@ -441,21 +463,17 @@
         yield 3
         m0.wait_recv()
         here = halves(block(1), 0)
-        f0 = net.start(here, here, up, n)
+        net.start(here, here, up, n, n)
         p1.wait_recv()
         here = halves(block(2), 1)
-        f1 = net.start(here, here, down, n)
+        net.start(here, here, down, n, n)
         yield
         m1.wait_recv()
-        if not brief:
-            yield 1
+        yield 1
         p0.wait_recv()
-        if not brief:
-            yield 2
-        f0.wait_recv()
-        f1.wait_recv()
-        if not brief:
-            yield 0
+        yield 2
+        net.arrived(n, mine)
+        yield 0
 
     def large(n, dim, k0, item, ready):
         up, down = at.step(dim, 1), at.step(dim, 3)
@@ -499,9 +517,9 @@
             yield
 
     def colour_a():
-        f_a[pl.ds(BLOCK, GROUP), :] = jnp.zeros((GROUP, WA), F32)
-        yield from later("ma", "y", lambda j: item_a(own_a, x, j), by_cols(WA // 2), s1a, s2a, first("a"), GROUP, f_a)
-        spread("a", f_a, OWN_A, GROUP, snd_a, rcv_a)
+        pk_a[...] = jnp.zeros(pk_a.shape, F32)
+        yield from later("ma", "y", lambda j: item_a(own_a, x, j), by_cols(WA // 2), s1a, s2a, first("a"), 0, GROUP, f_a)
+        spread("a", f_a, OWN_A, pk_a, snd_a, rcv_a)
         yield
         net.arrived("sa", rcv_a.at[pl.ds(0, OTHERS)])
         step_a()
@@ -513,9 +531,9 @@
         yield from large("a", "x", x, out, small("ga", "y", lambda j: out(x, j), by_cols(WA // 2)))
 
     def colour_b():
-        f_b[pl.ds(TALL, GROUP), :] = jnp.zeros((GROUP, D), F32)
-        yield from later("mb", "x", lambda j: item_b(own_b, y, j), by_rows(104, 96), s1b, s2b, first("b"), BLOCK, f_b)
-        spread("b", f_b, OWN_B, 32, snd_b, rcv_b)
+        pk_b[...] = jnp.zeros(pk_b.shape, F32)
+        yield from later("mb", "x", lambda j: item_b(own_b, y, j), by_rows(104, 96), s1b, s2b, first("b"), 13, BLOCK, f_b)
+        spread("b", f_b, OWN_B, pk_b, snd_b, rcv_b)
         yield
         net.arrived("sb", rcv_b.at[pl.ds(0, OTHERS)])
         step_b()
@@ -527,12 +545,16 @@
         yield from large("b", "y", y, out, small("gb", "x", lambda j: out(y, j), by_rows(104, 96)))
 
     def colour_c():
-        f_c[pl.ds(BLOCK, GROUP), :] = jnp.zeros((GROUP, WC), F32)
-        yield from later("mc", "x", lambda j: item_c(own_c, z, j), by_rows(80, 80), s1c, s2c, first("c"), 32, item_c(own_c, z, 3))
-        block = lambda j: own_c.at[z, rows(SLAB * x + BLOCK * rel(y, j), BLOCK), :]
-        split = by_cols(WC // 2) if WC % 256 == 0 else by_rows(24, 16)
-        yield from later("nc", "y", block, split, t1c, t2c, None, GROUP, f_c)
-        spread("c", f_c, OWN_A, GROUP, snd_c, rcv_c)
+        pk_c[...] = jnp.zeros(pk_c.shape, F32)
+        yield from later("mc", "x", lambda j: item_c(own_c, z, j), by_rows(80, 80), s1c, s2c, first("c"), 13, 32, item_c(own_c, z, 3))
+        part = lambda ref, yy: ref.at[z, rows(SLAB * x + BLOCK * yy, BLOCK), :]
+        for d in (1, 2, 3):
+            yy = lax.rem(y + d, 4)
+            net.start(part(own_c, yy), tc.at[d - 1], at.step("y", d), "nc", "nc")
+        yield
+        net.arrived("nc", tc)
+        vadd(f_c, (part(own_c, y), *(tc.at[d] for d in range(3))), BLOCK, GROUP)
+        spread("c", f_c, OWN_A, pk_c, snd_c, rcv_c)
         yield
         net.arrived("sc", rcv_c.at[pl.ds(0, OTHERS)])
         step_c()
@@ -540,16 +562,18 @@
         share("c", new_c, got_c)
         yield
         out = lambda k, j: item_c(o_c.at[c], k, j)
-        mine = lambda j: o_c.at[c, z, rows(SLAB * x + BLOCK * rel(y, j), BLOCK), :]
-        build("c", OWN_A, got_c, f_c, mine(3))
-        for _ in small("hc", "y", mine, split, True):
-            yield
+        mine = part(o_c.at[c], y)
+        build("c", OWN_A, got_c, f_c, mine)
+        for d in (1, 3, 2):
+            net.start(mine, mine, at.step("y", d), "hc", "hc")
+        yield
+        net.arrived("hc", tc)
         yield from large("c", "z", z, out, small("gc", "x", lambda j: out(z, j), by_rows(80, 80)))
 
     interleave(PLAN, release, c=colour_c(), a=colour_a(), b=colour_b(), p=prepare(), f=finish())
     for n, (own, *_) in colours.items():
         net.arrived("x" + n, own)
-    sizes = {"nc": own_c.at[0, pl.ds(0, 120), :], "hc": own_c.at[0, pl.ds(0, 120), :]}
+    sizes = {"nc": tc, "hc": tc}
     for n, (own, _, _, _, _, _, r, *_) in colours.items():
         sizes |= {"d" + n: own, "x" + n: own, "f" + n: r, "l" + n: r, "m" + n: r.at[pl.ds(0, 3)], "g" + n: r.at[pl.ds(0, 3)]}
     for n, rcv in (("a", rcv_a), ("b", rcv_b), ("c", rcv_c)):
@@ -567,11 +591,10 @@
     if UC:
         copies += [(c.at[l, k, :, pl.ds(WIN, UC)], up.at[l, :, pl.ds(UA + UC * k, UC)]) for l in range(2) for k in range(4)]
     copies += list(zip(small, outs, strict=True))
-    copies = [pltpu.make_async_copy(s, d, sem.at[i]) for i, (s, d) in enumerate(copies)]
-    for copy in copies:
-        copy.start()
-    for copy in copies:
-        copy.wait()
+    for src, dst in copies:
+        pltpu.make_async_copy(src, dst, sem).start()
+    for out in (gate, up, down, *outs):
+        pltpu.make_async_copy(out, out, sem).wait()
 
 
 def spec(space, n):
@@ -584,7 +607,8 @@
         turn = lambda one: jnp.transpose(one, (1, 0, 2))
         moments = [turn(one) for one in (*m, *v)]
         own_rows = [(2, GROUP, FF), (2, GROUP, FF), (2, 32, D)]
-        blocks = [(GROUP, GROUP, WA), (GROUP, 32, D), (GROUP, GROUP, WC)]
+        blocks = [(GROUP, PACK_A, LANES), (GROUP, PACK_B, LANES), (GROUP, PACK_C, LANES)]
+        states = [(2, PACK_A, LANES), (2, PACK_B, LANES), (2, 4, PACK_C, LANES)]
         results = pl.pallas_call(
             step_kernel,
             out_shape=[
@@ -606,27 +630,26 @@
                 VMEM((2, TALL, D), BF),
                 VMEM((2, 80, WC), BF),
                 VMEM((2, SLAB, WC), BF),
-                VMEM((2, BLOCK, WC // 2) if WC % 256 == 0 else (2, 24, WC), BF),
-                VMEM((2, BLOCK, WC), BF),
+                VMEM((3, BLOCK, WC), BF),
                 VMEM((BLOCK_PAD, WA), F32),
                 VMEM((TALL_PAD, D), F32),
                 VMEM((BLOCK_PAD, WC), F32),
                 *[VMEM(s, BF) for s in blocks] * 2,
-                VMEM((2, GROUP, WA), BF),
-                VMEM((2, 32, D), BF),
-                VMEM((2, GROUP, 4 * WC), BF),
+                *[VMEM(s, BF) for s in states],
                 *[VMEM(s, BF) for s in blocks],
                 VMEM((2, BLOCK, FF), BF),
                 VMEM((2, BLOCK, FF), BF),
                 VMEM((2, TALL, D), BF),
                 VMEM((BLOCK_PAD, FF), F32),
                 VMEM((TALL_PAD, D), F32),
+                *[VMEM(s, F32) for s in blocks],
+                *[VMEM(s, F32) for s in states] * 3,
                 *[VMEM(s, F32) for s in own_rows] * 3,
                 pltpu.SemaphoreType.DMA((SEND,)),
                 pltpu.SemaphoreType.DMA((RECV,)),
                 pltpu.SemaphoreType.DMA((LOCAL,)),
             ],
-            compiler_params=pltpu.CompilerParams(collective_id=0, has_side_effects=True, vmem_limit_bytes=34 * 2**20),
+            compiler_params=pltpu.CompilerParams(collective_id=0, has_side_effects=True, vmem_limit_bytes=36 * 2**20),
             name="step",
         )(*terms, *weights, *moments)
         done = pl.pallas_call(
@@ -634,7 +657,7 @@
             out_shape=[jax.ShapeDtypeStruct(w.shape, BF) for w in weights] + [jax.ShapeDtypeStruct(one.shape, F32) for one in moments],
             in_specs=spec(VMEM, 9),
             out_specs=spec(HBM, 9),
-            scratch_shapes=[pltpu.SemaphoreType.DMA((30,))],
+            scratch_shapes=[pltpu.SemaphoreType.DMA],
             compiler_params=pltpu.CompilerParams(vmem_limit_bytes=2**20),
             name="write",
         )(*results)

time: 147 us -> 134 us (0.912)
  Pallas kernels: 146 us -> 133 us
    pallas_call x1, Pallas kernels: 137 us -> 124 us  [step(): pl.pallas_call(step_kernel, out_shape=[VMEM((2, D, WA), BF), VMEM((2, FF,...]
where the time goes in v3:
time: 134 us; the launch traced here: 133 us
  Pallas kernels  133 us (99%)
    pallas_call x1, Pallas kernels, step(): pl.pallas_call(step_kernel, out_shape=[VMEM((2, D, WA), BF), VMEM((2, FF,...  124 us
    pallas_call x1, Pallas kernels, step(): pl.pallas_call(write_kernel, out_shape=[jax.ShapeDtypeStruct(w.shape, BF)...  8.48 us

profile of v3, /device:TPU:1, one launch (start us, length us, event | category | flops | bytes accessed | tf_op | source)
XLA Modules:
  0.0 133.5 jit_solution(15937934231199086086)
XLA Ops:
  0.6 124.3 %step.1 = (bf16[2,640,2816]{2,1,0:T(8,128)(2,1)S(1)}, bf16[2,3200,640]{2,1,0:T(8,128)(2,1)S(1)}, bf16[2,4,640,896]{3,2,1,0:T(8,128)(2,1)S(1)}, f32[5,2,3200]{2,1...) custom-call(bf16[1,2,640,3200]{3,2,1,0:T(8,128)(2,1)} %g_gate.1, ...), custom_call_target="tpu_custom_call" | custom-call | tf_op jit(solution)/shard_map/step/pallas_call | solution.py:612
  125.0 8.5 %write.1 = (bf16[2,640,3200]{2,1,0:T(8,128)(2,1)}, bf16[2,640,3200]{2,1,0:T(8,128)(2,1)}, bf16[2,3200,640]{2,1,0:T(8,128)(2,1)}, f32[5,2,3200]{2,1,0:T(2,128)}, ...) custom-call(bf16[2,640,2816]{2,1,0:T(8,128)(2,1)S(1)} %get-tuple-ele, ...), custom_call_target="tpu_custom_call" | custom-call | tf_op jit(solution)/shard_map/write/pallas_call | solution.py:655

commit v4 on v3

--- a/solution.py
+++ b/solution.py
@@ -18,9 +18,11 @@
 WA = UA + 128
 WC = 768 + UC
 PACK_A, PACK_B, PACK_C = 112, 128, 40
-PLAN = "cab" * 10 + "pppppppp" + "cab" * 2 + "pppppppppp" + "acb" * 2 + "aaaa" + "cbcb" + "cbcb"
-PLAN += "aacb" + "aA" + "cb" + "cb" + "cc" + "C" + "abB" + "abc" + "ABC" + "abc" + "ABC" + "abc" + "ABC"
-PLAN += "f" * 9
+PLAN = (
+    "cabcabcabcabcabcabcabcabcabcabppppppppcabcabpppp"
+    "ppppppacbacbaaaaccccbbbbacacaAbcabaAccCbBccCcCbb"
+    "BbBcCbBaAaAAfffffffff"
+)
 SEND, RECV, LOCAL = 26, 120, 34
 OFF = (2, 3, 1, 0)
 HBM = pltpu.MemorySpace.HBM
@@ -55,11 +57,11 @@
         return self.dev(**{dim: lax.rem(getattr(self, dim) + by, 4)})
 
     def group(self):
-        out = [(self.z, 1 - self.c)]
-        for dz in (1, 2, 3):
+        out = []
+        for dz in (2, 1, 3):
             zz = lax.rem(self.z + dz, 4)
             out += [(zz, self.c), (zz, 1 - self.c)]
-        return out
+        return [*out, (self.z, 1 - self.c)]
 
     def barrier(self):
         sem = pltpu.get_barrier_semaphore()
@@ -548,7 +550,7 @@
         pk_c[...] = jnp.zeros(pk_c.shape, F32)
         yield from later("mc", "x", lambda j: item_c(own_c, z, j), by_rows(80, 80), s1c, s2c, first("c"), 13, 32, item_c(own_c, z, 3))
         part = lambda ref, yy: ref.at[z, rows(SLAB * x + BLOCK * yy, BLOCK), :]
-        for d in (1, 2, 3):
+        for d in (2, 1, 3):
             yy = lax.rem(y + d, 4)
             net.start(part(own_c, yy), tc.at[d - 1], at.step("y", d), "nc", "nc")
         yield
@@ -564,7 +566,7 @@
         out = lambda k, j: item_c(o_c.at[c], k, j)
         mine = part(o_c.at[c], y)
         build("c", OWN_A, got_c, f_c, mine)
-        for d in (1, 3, 2):
+        for d in (2, 1, 3):
             net.start(mine, mine, at.step("y", d), "hc", "hc")
         yield
         net.arrived("hc", tc)

time: 134 us -> 132 us (0.985)
  Pallas kernels: 133 us -> 131 us
    pallas_call x1, Pallas kernels: 124 us -> 123 us  [step(): pl.pallas_call(step_kernel, out_shape=[VMEM((2, D, WA), BF), VMEM((2, FF,...]
where the time goes in v4:
time: 132 us
  Pallas kernels  131 us (99%)
    pallas_call x1, Pallas kernels, step(): pl.pallas_call(step_kernel, out_shape=[VMEM((2, D, WA), BF), VMEM((2, FF,...  123 us
    pallas_call x1, Pallas kernels, step(): pl.pallas_call(write_kernel, out_shape=[jax.ShapeDtypeStruct(w.shape, BF)...  8.48 us

profile of v4, /device:TPU:1, one launch (start us, length us, event | category | flops | bytes accessed | tf_op | source)
XLA Modules:
  0.0 132.1 jit_solution(6876521945477327677)
XLA Ops:
  0.6 122.9 %step.1 = (bf16[2,640,2816]{2,1,0:T(8,128)(2,1)S(1)}, bf16[2,3200,640]{2,1,0:T(8,128)(2,1)S(1)}, bf16[2,4,640,896]{3,2,1,0:T(8,128)(2,1)S(1)}, f32[5,2,3200]{2,1...) custom-call(bf16[1,2,640,3200]{3,2,1,0:T(8,128)(2,1)} %g_gate.1, ...), custom_call_target="tpu_custom_call" | custom-call | tf_op jit(solution)/shard_map/step/pallas_call | solution.py:614
  123.6 8.5 %write.1 = (bf16[2,640,3200]{2,1,0:T(8,128)(2,1)}, bf16[2,640,3200]{2,1,0:T(8,128)(2,1)}, bf16[2,3200,640]{2,1,0:T(8,128)(2,1)}, f32[5,2,3200]{2,1,0:T(2,128)}, ...) custom-call(bf16[2,640,2816]{2,1,0:T(8,128)(2,1)S(1)} %get-tuple-ele, ...), custom_call_target="tpu_custom_call" | custom-call | tf_op jit(solution)/shard_map/write/pallas_call | solution.py:657
